TPU v7x, 32 devices: a whole 2x2x4 slice. The times are simulated.
32 devices in a mesh: grp: 2 (over x), seq: 16 (over z, y, core).
Axes of the slice: x: 2, y: 2, z: 4, core: 2. Of those that a mesh axis runs over, the one named last changes fastest.
Arguments:
- queries: bfloat16 [256, 4096], P(('grp', 'seq')), parts along dimension 0, may hold values from -9 to 9
- question_keys: bfloat16 [256, 2048], P(('grp', 'seq')), parts along dimension 0, may hold values from -4 to 4
- question_values: bfloat16 [256, 2048], P(('grp', 'seq')), parts along dimension 0, may hold values from -5 to 5
- doc_keys: bfloat16 [16384, 2048], P(('grp', 'seq')), parts along dimension 0, may hold values from -4 to 4
- doc_values: bfloat16 [16384, 2048], P(('grp', 'seq')), parts along dimension 0, may hold values from -5 to 5
- lengths: int32 [2], P('grp'), parts along dimension 0, may hold values from 4 to 128
- offsets: int32 [2], P('grp'), parts along dimension 0, may hold values from 2 to 8192, as said below
Outputs:
- attended: bfloat16 [256, 4096], P(('grp', 'seq')), parts along dimension 0
There are 2 independent parts, one for each index of `grp`. A program takes and returns all parts, laid end to end along the dimension named above; each array names one. Nothing has to cross between parts.
Inputs may be any that keep to these rules, and one draw needn't show every extreme that they name: Some question has offsets equal to 8192.
All inputs are finite; a program needn't handle non-finite values.
Results may differ from a plain program's by a relative error of at most 0.0029.
Values may be sent and summed in bfloat16 or wider, within the bound.
A program may use at most 64 MiB of HBM per device.

v0:
```python
import functools
import math

import jax
import jax.numpy as jnp
from jax import lax
from jax.experimental import pallas as pl
from jax.experimental.pallas import tpu as pltpu
from jax.sharding import PartitionSpec as P

H = 32
KVH = 16
HD = 128
QSCALE = 144
QL = 128
NQ = 1


MASKED = -1e30


def row_tables(start, count, lengths, offsets):
    rows = start + jnp.arange(count, dtype=jnp.int32)
    question = rows // QL
    position = rows % QL
    owner_table = question[:, None] == jnp.arange(NQ, dtype=jnp.int32)[None, :]
    row_length = jnp.sum(jnp.where(owner_table, lengths[None, :], 0), axis=1)
    row_offset = jnp.sum(jnp.where(owner_table, offsets[None, :], 0), axis=1)
    return (question, position, position < row_length, row_offset)


def local(queries, question_keys, question_values, doc_keys, doc_values, lengths, offsets):
    rows_local = queries.shape[0]
    doc_local = doc_keys.shape[0]
    device_count = lax.axis_size("seq")
    device_index = lax.axis_index("seq")
    total_rows = rows_local * device_count
    per_group = H // KVH
    factor_q = QSCALE ** (-0.5)
    key_doc = doc_keys.reshape(doc_local, KVH, HD)
    value_doc = doc_values.reshape(doc_local, KVH, HD)
    key_self = question_keys.reshape(rows_local, KVH, HD)
    value_self = question_values.reshape(rows_local, KVH, HD)
    doc_places = device_index * doc_local + jnp.arange(doc_local, dtype=jnp.int32)
    self_rows = device_index * rows_local + jnp.arange(rows_local, dtype=jnp.int32)
    whole = lax.all_gather(queries, "seq", axis=0, tiled=True)
    block_rows = math.gcd(total_rows, 512)
    block_count = total_rows // block_rows

    def one_block(start):
        piece = whole.reshape(block_rows, KVH, per_group, HD)
        question, position, live_rows, row_offset = row_tables(start, block_rows, lengths, offsets)
        mask_doc = live_rows[:, None] & (doc_places[None, :] < row_offset[:, None])
        mask_self = (
            live_rows[:, None]
            & (self_rows[None, :] // QL == question[:, None])
            & (self_rows[None, :] % QL <= position[:, None])
        )
        mask_doc = mask_doc[:, None, None, :]
        mask_self = mask_self[:, None, None, :]
        scores_doc = (
            jnp.einsum("rgjd,kgd->rgjk", piece, key_doc, preferred_element_type=jnp.float32)
            * factor_q
        )
        scores_self = (
            jnp.einsum("rgjd,kgd->rgjk", piece, key_self, preferred_element_type=jnp.float32)
            * factor_q
        )
        scores_doc = jnp.where(mask_doc, scores_doc, MASKED)
        scores_self = jnp.where(mask_self, scores_self, MASKED)
        block_top = jnp.maximum(jnp.max(scores_doc, axis=-1), jnp.max(scores_self, axis=-1))
        weights_doc = jnp.where(mask_doc, jnp.exp(scores_doc - block_top[..., None]), 0.0).astype(
            jnp.bfloat16
        )
        weights_self = jnp.where(
            mask_self, jnp.exp(scores_self - block_top[..., None]), 0.0
        ).astype(jnp.bfloat16)
        block_den = jnp.sum(weights_doc.astype(jnp.float32), axis=-1) + jnp.sum(
            weights_self.astype(jnp.float32), axis=-1
        )
        block_num = jnp.einsum(
            "rgjk,kgd->rgjd", weights_doc, value_doc, preferred_element_type=jnp.float32
        )
        block_num = block_num + jnp.einsum(
            "rgjk,kgd->rgjd", weights_self, value_self, preferred_element_type=jnp.float32
        )
        return (
            block_num.reshape(block_rows, H * HD),
            block_top.reshape(block_rows, H),
            block_den.reshape(block_rows, H),
        )

    starts = jnp.arange(block_count, dtype=jnp.int32) * block_rows
    numer, row_top, denom = lax.map(one_block, starts)
    numer = numer.reshape(total_rows, H * HD)
    row_top = row_top.reshape(total_rows, H)
    denom = denom.reshape(total_rows, H)
    got_num, got_top, got_den = (
        lax.all_to_all(numer[None], "seq", split_axis=1, concat_axis=0, tiled=True),
        lax.all_to_all(row_top[None], "seq", split_axis=1, concat_axis=0, tiled=True),
        lax.all_to_all(denom[None], "seq", split_axis=1, concat_axis=0, tiled=True),
    )
    overall = jnp.max(got_top, axis=0)
    rescale = jnp.exp(got_top - overall[None])
    total_num = jnp.sum(
        got_num.reshape(device_count, rows_local, H, HD) * rescale[:, :, :, None], axis=0
    )
    total_den = jnp.sum(got_den * rescale, axis=0)
    question, position, live_rows, row_offset = row_tables(
        device_index * rows_local, rows_local, lengths, offsets
    )
    safe_den = jnp.where(live_rows[:, None], total_den, 1.0)
    result = (total_num / safe_den[:, :, None]).reshape(rows_local, H * HD)
    return jnp.where(live_rows[:, None], result, 0.0).astype(jnp.bfloat16)


MESH = pl.DeviceIdType.MESH
LANE = 128
CHUNKS = 4
LOG2E = math.log2(math.e)
WIRE = jnp.int16
WIRE_TOP = 32767.0


def fused_kernel(
    n, q_ref, qk_ref, qv_ref, k_hbm, v_hbm, len_ref, off_ref, o_ref,
    kbuf, vbuf, bias, qbuf, nkeep, skeep, nsend, ssend, narr, sarr, wsend, wstat, warr, wsarr,
    kv_sem, q_send, q_recv, f_send, f_recv, p_send, p_recv, w_send, w_recv,
):
    chips = n // 2
    rows = q_ref.shape[0]
    doc = k_hbm.shape[0]
    keys = kbuf.shape[0]
    half = chips * rows
    total = 2 * half
    group_width = (KVH // CHUNKS) * HD
    wide = (H // CHUNKS) * HD
    heads = H // CHUNKS
    per_group = H // KVH
    me = lax.axis_index("seq")
    chip, core = me // 2, me % 2
    partner = chip * 2 + 1 - core

    def peer(d):
        return lax.rem(chip + d, chips)

    def kv_copies(c):
        cols = pl.ds(c * group_width, group_width)
        return (
            pltpu.make_async_copy(k_hbm.at[:, cols], kbuf.at[pl.ds(0, doc), cols], kv_sem.at[0, c]),
            pltpu.make_async_copy(v_hbm.at[:, cols], vbuf.at[pl.ds(0, doc), cols], kv_sem.at[1, c]),
        )

    for c in range(CHUNKS):
        for copy in kv_copies(c):
            copy.start()
    barrier = pltpu.get_barrier_semaphore()
    for d in range(1, n):
        pl.semaphore_signal(
            barrier, inc=1, device_id={"seq": lax.rem(me + d, n)}, device_id_type=MESH
        )

    for buf, own in ((kbuf, qk_ref), (vbuf, qv_ref)):
        wide_own = own[...].astype(jnp.float32)
        pad = jnp.zeros((keys - doc - rows, own.shape[1]), jnp.float32)
        buf[doc:, :] = jnp.concatenate([wide_own, pad], axis=0).astype(buf.dtype)
    for c in range(CHUNKS):
        qbuf[c, 0, chip] = q_ref[:, c * wide : (c + 1) * wide]
    slot = lax.broadcasted_iota(jnp.int32, (total, keys), 0)
    place = lax.broadcasted_iota(jnp.int32, (total, keys), 1)
    side = slot // half
    inner = slot % half
    row = (2 * (inner // rows) + jnp.where(side == 0, core, 1 - core)) * rows + inner % rows
    question, position = row // QL, row % QL
    row_length = jnp.zeros_like(row)
    row_offset = jnp.zeros_like(row)
    for i in range(NQ):
        row_length = jnp.where(question == i, len_ref[i], row_length)
        row_offset = jnp.where(question == i, off_ref[i], row_offset)
    self_row = me * rows + place - doc
    seen_doc = (place < doc) & (me * doc + place < row_offset)
    seen_self = (
        (place >= doc) & (place < doc + rows)
        & (self_row // QL == question) & (self_row % QL <= position)
    )
    bias[...] = jnp.where((position < row_length) & (seen_doc | seen_self), 0.0, MASKED)
    pl.semaphore_wait(barrier, n - 1)

    def q_copy(c, d):
        return pltpu.make_async_remote_copy(
            q_ref.at[:, pl.ds(c * wide, wide)], qbuf.at[c, 0, chip],
            q_send.at[c, d], q_recv.at[c, d],
            device_id={"seq": peer(d) * 2 + core}, device_id_type=MESH,
        )

    def f_copy(c, d):
        source = q_ref.at[:, pl.ds(c * wide, wide)] if d == 0 else qbuf.at[c, 0, peer(chips - d)]
        return pltpu.make_async_remote_copy(
            source, qbuf.at[c, 1, peer(chips - d)], f_send.at[c, d], f_recv.at[c, d],
            device_id={"seq": partner}, device_id_type=MESH,
        )

    def p_copies(c):
        return tuple(
            pltpu.make_async_remote_copy(
                a.at[c], b.at[c], p_send.at[c, i], p_recv.at[c, i],
                device_id={"seq": partner}, device_id_type=MESH,
            )
            for i, (a, b) in enumerate(((nsend, narr), (ssend, sarr)))
        )

    def w_copy(c, d):
        return pltpu.make_async_remote_copy(
            wsend.at[c, peer(d)], warr.at[c, chip], w_send.at[c, d], w_recv.at[c, d],
            device_id={"seq": peer(d) * 2 + core}, device_id_type=MESH,
        )

    def s_copy(d):
        return pltpu.make_async_remote_copy(
            wstat.at[peer(d)], wsarr.at[chip], w_send.at[CHUNKS, d], w_recv.at[CHUNKS, d],
            device_id={"seq": peer(d) * 2 + core}, device_id_type=MESH,
        )

    for c in range(CHUNKS):
        f_copy(c, 0).start()
        for d in range(1, chips):
            q_copy(c, d).start()

    factor = QSCALE ** (-0.5) * LOG2E

    def attend(c):
        for g in range(KVH // CHUNKS):
            cols = slice(c * group_width + g * HD, c * group_width + (g + 1) * HD)
            key, value = kbuf[:, cols], vbuf[:, cols]
            pieces = []
            for j in range(per_group):
                h = g * per_group + j
                block = qbuf[c, :, :, :, h * HD : (h + 1) * HD].astype(jnp.float32)
                pieces.append(block.reshape(total, HD).astype(jnp.bfloat16))
            query = jnp.concatenate(pieces, axis=0)
            scores = lax.dot_general(
                query, key, (((1,), (1,)), ((), ())), preferred_element_type=jnp.float32
            )
            for j in range(per_group):
                h = g * per_group + j
                part = scores[j * total : (j + 1) * total] * factor + bias[...]
                top = jnp.max(part, axis=1, keepdims=True)
                weights = jnp.exp2(part - top).astype(jnp.bfloat16)
                den = jnp.sum(weights.astype(jnp.float32), axis=1, keepdims=True)
                num = jnp.dot(weights, value, preferred_element_type=jnp.float32)
                hc = slice(h * HD, (h + 1) * HD)
                nkeep[c, :, hc] = num[:half]
                nsend[c, :, hc] = num[half:]
                for stat, buf in ((top, 0), (den, heads)):
                    skeep[c, :, buf + h : buf + h + 1] = stat[:half]
                    ssend[c, :, buf + h : buf + h + 1] = stat[half:]

    def pair_up(c):
        for copy in p_copies(c):
            copy.wait_recv()
        stat_a, stat_b = skeep[c], sarr[c]
        top_a, top_b = stat_a[:, :heads], stat_b[:, :heads]
        top = jnp.maximum(top_a, top_b)
        fa, fb = jnp.exp2(top_a - top), jnp.exp2(top_b - top)
        den = stat_a[:, heads : 2 * heads] * fa + stat_b[:, heads : 2 * heads] * fb
        for h in range(heads):
            hc = slice(h * HD, (h + 1) * HD)
            num = nkeep[c, :, hc] * fa[:, h : h + 1] + narr[c, :, hc] * fb[:, h : h + 1]
            largest = jnp.maximum(jnp.max(jnp.abs(num), axis=1, keepdims=True), 1e-30)
            wsend[c, :, :, hc] = encode(num / largest).reshape(chips, rows, HD)
            for kind, stat in enumerate((top[:, h : h + 1], den[:, h : h + 1], largest)):
                at = (c * 3 + kind) * heads + h
                wstat[:, :, at : at + 1] = stat.reshape(chips, rows, 1)
        for d in range(1, chips):
            if c == CHUNKS - 1:
                s_copy(d).start()
            w_copy(c, d).start()
        warr[c, chip] = wsend[c, chip]
        if c == CHUNKS - 1:
            wsarr[chip] = wstat[chip]

    for c in range(CHUNKS):
        for d in range(1, chips):
            q_copy(c, d).wait_recv()
            f_copy(c, d).start()
        for d in range(chips):
            f_copy(c, d).wait_recv()
        for copy in kv_copies(c):
            copy.wait()
        attend(c)
        for copy in p_copies(c):
            copy.start()
        if c > 0:
            pair_up(c - 1)
    pair_up(CHUNKS - 1)

    mine = me * rows + lax.broadcasted_iota(jnp.int32, (rows, HD), 0)
    live_to = jnp.zeros_like(mine)
    for i in range(NQ):
        live_to = jnp.where(mine // QL == i, len_ref[i], live_to)
    live = mine % QL < live_to
    for d in range(1, chips):
        s_copy(d).wait_recv()
    for c in range(CHUNKS):
        for d in range(1, chips):
            w_copy(c, d).wait_recv()
        top_at, den_at, scale_at = ((c * 3 + kind) * heads for kind in range(3))
        tops = [wsarr[k][:, top_at : top_at + heads] for k in range(chips)]
        overall = functools.reduce(jnp.maximum, tops)
        shrink = [jnp.exp2(t - overall) for t in tops]
        den = sum(wsarr[k][:, den_at : den_at + heads] * shrink[k] for k in range(chips))
        coefs = [wsarr[k][:, scale_at : scale_at + heads] * shrink[k] / den for k in range(chips)]
        for h in range(heads):
            hc = slice(h * HD, (h + 1) * HD)
            acc = jnp.zeros((rows, HD), jnp.float32)
            for k in range(chips):
                acc = acc + decode(warr[c, k, :, hc]) * coefs[k][:, h : h + 1]
            o_ref[:, c * wide + h * HD : c * wide + (h + 1) * HD] = jnp.where(live, acc, 0.0).astype(
                o_ref.dtype
            )
    for c in range(CHUNKS):
        f_copy(c, 0).wait_send()
        for d in range(1, chips):
            q_copy(c, d).wait_send()
            f_copy(c, d).wait_send()
            w_copy(c, d).wait_send()
        for copy in p_copies(c):
            copy.wait_send()
    for d in range(1, chips):
        s_copy(d).wait_send()


def encode(x):
    return jnp.round(x * WIRE_TOP).astype(jnp.int32).astype(WIRE)


def decode(x):
    return x.astype(jnp.int32).astype(jnp.float32) * (1.0 / WIRE_TOP)


def fused(n, queries, question_keys, question_values, doc_keys, doc_values, lengths, offsets):
    rows = queries.shape[0]
    doc = doc_keys.shape[0]
    if rows % 8 or n % 2 or n * rows > 256 or doc % LANE or doc > 1024 or 3 * H > LANE:
        return local(
            queries, question_keys, question_values, doc_keys, doc_values, lengths, offsets
        )
    chips = n // 2
    half = chips * rows
    keys = doc + -(-rows // LANE) * LANE
    wide = H * HD // CHUNKS
    vmem = pl.BlockSpec(memory_space=pltpu.VMEM)
    smem = pl.BlockSpec(memory_space=pltpu.SMEM)
    hbm = pl.BlockSpec(memory_space=pl.ANY)
    f32 = jnp.float32
    dma = pltpu.SemaphoreType.DMA
    return pl.pallas_call(
        functools.partial(fused_kernel, n),
        out_shape=jax.ShapeDtypeStruct(queries.shape, jnp.bfloat16),
        in_specs=[vmem, vmem, vmem, hbm, hbm, smem, smem],
        out_specs=vmem,
        scratch_shapes=[
            pltpu.VMEM((keys, KVH * HD), jnp.bfloat16),
            pltpu.VMEM((keys, KVH * HD), jnp.bfloat16),
            pltpu.VMEM((2 * half, keys), f32),
            pltpu.VMEM((CHUNKS, 2, chips, rows, wide), jnp.bfloat16),
            pltpu.VMEM((CHUNKS, half, wide), f32),
            pltpu.VMEM((CHUNKS, half, LANE), f32),
            pltpu.VMEM((CHUNKS, half, wide), f32),
            pltpu.VMEM((CHUNKS, half, LANE), f32),
            pltpu.VMEM((CHUNKS, half, wide), f32),
            pltpu.VMEM((CHUNKS, half, LANE), f32),
            pltpu.VMEM((CHUNKS, chips, rows, wide), WIRE),
            pltpu.VMEM((chips, rows, LANE), f32),
            pltpu.VMEM((CHUNKS, chips, rows, wide), WIRE),
            pltpu.VMEM((chips, rows, LANE), f32),
            dma((2, CHUNKS)),
            dma((CHUNKS, chips)),
            dma((CHUNKS, chips)),
            dma((CHUNKS, chips)),
            dma((CHUNKS, chips)),
            dma((CHUNKS, 2)),
            dma((CHUNKS, 2)),
            dma((CHUNKS + 1, chips)),
            dma((CHUNKS + 1, chips)),
        ],
        compiler_params=pltpu.CompilerParams(
            collective_id=0, has_side_effects=True, vmem_limit_bytes=60 * 1024 * 1024
        ),
    )(queries, question_keys, question_values, doc_keys, doc_values, lengths, offsets)


def solution(mesh):
    placed = (
        P(("grp", "seq"), None),
        P(("grp", "seq"), None),
        P(("grp", "seq"), None),
        P(("grp", "seq"), None),
        P(("grp", "seq"), None),
        P("grp"),
        P("grp"),
    )
    return jax.shard_map(
        functools.partial(fused, mesh.shape["seq"]),
        mesh=mesh, in_specs=placed, out_specs=P(("grp", "seq"), None), check_vma=False,
    )
```

profile of v0, /device:TPU:0, one launch (start us, length us, event | category | flops | bytes accessed | tf_op | source)
XLA Modules:
  0.0 40.8 jit_solution(8188790791552631396)
XLA Ops:
  1.3 38.1 %shard_map.73 = bf16[8,4096]{1,0:T(8,128)(2,1)} custom-call(bf16[8,4096]{1,0:T(8,128)(2,1)} %q_ref.1, bf16[8,2048]{1,0:T(8,128)(2,1)} %qk_ref.1, bf16[8,2048]{1,0:T(8,128)(2,1)} %qv_ref.1, bf16[512,2048]{1,0:T(8,128)(2,1)} %k_hbm.1, bf16[512,2048]{1,0:T(8,128)(2,1)} %v_hbm.1, s32[1]{0:T(128)S(6)} %copy.9.len_ref, s32[1]{0:T(128)S(6)} %copy.10.off_ref), custom_call_target="tpu_custom_call" | custom-call | tf_op jit(solution)/shard_map/pallas_call | solution.py:357
  39.4 1.5 %copy.11 = bf16[8,4096]{1,0:T(8,128)(2,1)} copy(bf16[8,4096]{1,0:T(8,128)(2,1)} %shard_map.73) | data formatting | bytes 131072
where the time goes:
time: 41.1 us; the launch traced here: 40.8 us
  Pallas kernels  38.1 us (93%)
  local copies, waits for them, and re-layouts  1.47 us (4%)
  between operations  1.3 us (3%)
    pallas_call x1, Pallas kernels, fused(): pl.pallas_call(functools.partial(fused_kernel, n), out_shape=jax.ShapeDty...  38.1 us
    unnamed x1, local copies, waits for them, and re-layouts  1.47 us

commit v1 on v0

v1 whole, which is shorter than its diff:
```python
import functools
import math

import jax
import jax.numpy as jnp
from jax import lax
from jax.experimental import pallas as pl
from jax.experimental.pallas import tpu as pltpu
from jax.sharding import PartitionSpec as P

H = 32
KVH = 16
HD = 128
QSCALE = 144
QL = 128
NQ = 1


MASKED = -1e30


def row_tables(start, count, lengths, offsets):
    rows = start + jnp.arange(count, dtype=jnp.int32)
    question = rows // QL
    position = rows % QL
    owner_table = question[:, None] == jnp.arange(NQ, dtype=jnp.int32)[None, :]
    row_length = jnp.sum(jnp.where(owner_table, lengths[None, :], 0), axis=1)
    row_offset = jnp.sum(jnp.where(owner_table, offsets[None, :], 0), axis=1)
    return (question, position, position < row_length, row_offset)


def local(queries, question_keys, question_values, doc_keys, doc_values, lengths, offsets):
    rows_local = queries.shape[0]
    doc_local = doc_keys.shape[0]
    device_count = lax.axis_size("seq")
    device_index = lax.axis_index("seq")
    total_rows = rows_local * device_count
    per_group = H // KVH
    factor_q = QSCALE ** (-0.5)
    key_doc = doc_keys.reshape(doc_local, KVH, HD)
    value_doc = doc_values.reshape(doc_local, KVH, HD)
    key_self = question_keys.reshape(rows_local, KVH, HD)
    value_self = question_values.reshape(rows_local, KVH, HD)
    doc_places = device_index * doc_local + jnp.arange(doc_local, dtype=jnp.int32)
    self_rows = device_index * rows_local + jnp.arange(rows_local, dtype=jnp.int32)
    whole = lax.all_gather(queries, "seq", axis=0, tiled=True)
    block_rows = math.gcd(total_rows, 512)
    block_count = total_rows // block_rows

    def one_block(start):
        piece = whole.reshape(block_rows, KVH, per_group, HD)
        question, position, live_rows, row_offset = row_tables(start, block_rows, lengths, offsets)
        mask_doc = live_rows[:, None] & (doc_places[None, :] < row_offset[:, None])
        mask_self = (
            live_rows[:, None]
            & (self_rows[None, :] // QL == question[:, None])
            & (self_rows[None, :] % QL <= position[:, None])
        )
        mask_doc = mask_doc[:, None, None, :]
        mask_self = mask_self[:, None, None, :]
        scores_doc = (
            jnp.einsum("rgjd,kgd->rgjk", piece, key_doc, preferred_element_type=jnp.float32)
            * factor_q
        )
        scores_self = (
            jnp.einsum("rgjd,kgd->rgjk", piece, key_self, preferred_element_type=jnp.float32)
            * factor_q
        )
        scores_doc = jnp.where(mask_doc, scores_doc, MASKED)
        scores_self = jnp.where(mask_self, scores_self, MASKED)
        block_top = jnp.maximum(jnp.max(scores_doc, axis=-1), jnp.max(scores_self, axis=-1))
        weights_doc = jnp.where(mask_doc, jnp.exp(scores_doc - block_top[..., None]), 0.0).astype(
            jnp.bfloat16
        )
        weights_self = jnp.where(
            mask_self, jnp.exp(scores_self - block_top[..., None]), 0.0
        ).astype(jnp.bfloat16)
        block_den = jnp.sum(weights_doc.astype(jnp.float32), axis=-1) + jnp.sum(
            weights_self.astype(jnp.float32), axis=-1
        )
        block_num = jnp.einsum(
            "rgjk,kgd->rgjd", weights_doc, value_doc, preferred_element_type=jnp.float32
        )
        block_num = block_num + jnp.einsum(
            "rgjk,kgd->rgjd", weights_self, value_self, preferred_element_type=jnp.float32
        )
        return (
            block_num.reshape(block_rows, H * HD),
            block_top.reshape(block_rows, H),
            block_den.reshape(block_rows, H),
        )

    starts = jnp.arange(block_count, dtype=jnp.int32) * block_rows
    numer, row_top, denom = lax.map(one_block, starts)
    numer = numer.reshape(total_rows, H * HD)
    row_top = row_top.reshape(total_rows, H)
    denom = denom.reshape(total_rows, H)
    got_num, got_top, got_den = (
        lax.all_to_all(numer[None], "seq", split_axis=1, concat_axis=0, tiled=True),
        lax.all_to_all(row_top[None], "seq", split_axis=1, concat_axis=0, tiled=True),
        lax.all_to_all(denom[None], "seq", split_axis=1, concat_axis=0, tiled=True),
    )
    overall = jnp.max(got_top, axis=0)
    rescale = jnp.exp(got_top - overall[None])
    total_num = jnp.sum(
        got_num.reshape(device_count, rows_local, H, HD) * rescale[:, :, :, None], axis=0
    )
    total_den = jnp.sum(got_den * rescale, axis=0)
    question, position, live_rows, row_offset = row_tables(
        device_index * rows_local, rows_local, lengths, offsets
    )
    safe_den = jnp.where(live_rows[:, None], total_den, 1.0)
    result = (total_num / safe_den[:, :, None]).reshape(rows_local, H * HD)
    return jnp.where(live_rows[:, None], result, 0.0).astype(jnp.bfloat16)


MESH = pl.DeviceIdType.MESH
LANE = 128
CHUNKS = 4
LOG2E = math.log2(math.e)
WIRE = jnp.int16
WIRE_TOP = 32767.0
HALF_KVH = KVH // 2
PER_GROUP = H // KVH
GROUPS = HALF_KVH // CHUNKS
STATS = 8


def fused_kernel(
    n, q_hbm, qk_hbm, qv_hbm, k_hbm, v_hbm, len_hbm, off_hbm, o_ref,
    qown, qbuf, kself, vself, kbuf, vt, bias_doc, bias_self, scores, len_ref, off_ref, vbuf,
    nkeep, skeep, nsend, ssend, narr, sarr, wsend, wstat, warr, wsarr,
    q_sem, in_sem, kv_sem, kv_send, kv_recv,
    zq_send, zq_recv, yq_send, yq_recv, pq_send, pq_recv, f_send, f_recv,
    p_send, p_recv, w_send, w_recv,
):
    length = n // 4
    rows = q_hbm.shape[0]
    doc = k_hbm.shape[0]
    docs = 2 * doc
    selves = 2 * rows
    half_kv = HALF_KVH * HD
    half_q = half_kv * PER_GROUP
    kv_wide = GROUPS * HD
    wide = kv_wide * PER_GROUP
    side = length * 2 * rows
    me = lax.axis_index("seq")
    core = lax.rem(me, 2)
    chip = me // 2
    y = lax.rem(chip, 2)
    z = chip // 2

    def device(zz, yy, cc):
        return {"seq": (zz * 2 + yy) * 2 + cc}

    def zpeer(d):
        return lax.rem(z + d, length)

    barrier = pltpu.get_barrier_semaphore()
    peers = [device(z, y, 1 - core)] + [device(z, 1 - y, cc) for cc in range(2)]
    peers += [device(zpeer(d), y, cc) for d in range(1, length) for cc in range(2)]
    for peer in peers:
        pl.semaphore_signal(barrier, inc=1, device_id=peer, device_id_type=MESH)

    q_in = pltpu.make_async_copy(q_hbm, qown, q_sem.at[CHUNKS])
    q_in.start()
    small = [
        pltpu.make_async_copy(len_hbm, len_ref, in_sem.at[0]),
        pltpu.make_async_copy(off_hbm, off_ref, in_sem.at[1]),
        pltpu.make_async_copy(qk_hbm.at[:, pl.ds(core * half_kv, half_kv)], kself.at[core], in_sem.at[2]),
        pltpu.make_async_copy(qv_hbm.at[:, pl.ds(core * half_kv, half_kv)], vself.at[core], in_sem.at[3]),
    ]
    for copy in small:
        copy.start()

    def q_own(c):
        return pltpu.make_async_copy(
            q_hbm.at[:, pl.ds(core * half_q + c * wide, wide)], qbuf.at[c, y, z, core], q_sem.at[c]
        )

    def kv_local(c):
        cols = pl.ds(core * half_kv + c * kv_wide, kv_wide)
        at = pl.ds(core * doc, doc)
        to = pl.ds(c * kv_wide, kv_wide)
        return (
            pltpu.make_async_copy(k_hbm.at[:, cols], kbuf.at[at, to], kv_sem.at[0, c]),
            pltpu.make_async_copy(v_hbm.at[:, cols], vbuf.at[at, to], kv_sem.at[1, c]),
        )

    def kv_remote(c):
        cols = pl.ds((1 - core) * half_kv + c * kv_wide, kv_wide)
        at = pl.ds(core * doc, doc)
        to = pl.ds(c * kv_wide, kv_wide)
        return tuple(
            pltpu.make_async_remote_copy(
                a.at[:, cols], b.at[at, to], kv_send.at[i, c], kv_recv.at[i, c],
                device_id=device(z, y, 1 - core), device_id_type=MESH,
            )
            for i, (a, b) in enumerate(((k_hbm, kbuf), (v_hbm, vbuf)))
        )

    def self_remote():
        cols = pl.ds((1 - core) * half_kv, half_kv)
        return tuple(
            pltpu.make_async_remote_copy(
                a.at[:, cols], b.at[core], kv_send.at[i, CHUNKS], kv_recv.at[i, CHUNKS],
                device_id=device(z, y, 1 - core), device_id_type=MESH,
            )
            for i, (a, b) in enumerate(((qk_hbm, kself), (qv_hbm, vself)))
        )

    def q_piece(c, cc):
        return qown.at[:, pl.ds(cc * half_q + c * wide, wide)]

    def zq(c, d, cc):
        return pltpu.make_async_remote_copy(
            q_piece(c, cc), qbuf.at[c, y, z, core], zq_send.at[c, d, cc], zq_recv.at[c, d, core],
            device_id=device(zpeer(d), y, cc), device_id_type=MESH,
        )

    def zq_wait(c, d):
        for cc in range(2):
            pltpu.make_async_remote_copy(
                q_piece(c, cc), qbuf.at[c, y, zpeer(length - d), cc],
                zq_send.at[c, d, cc], zq_recv.at[c, d, cc],
                device_id=device(zpeer(d), y, cc), device_id_type=MESH,
            ).wait_recv()

    def yq(c, cc):
        return pltpu.make_async_remote_copy(
            q_piece(c, cc), qbuf.at[c, y, z, core], yq_send.at[c, cc], yq_recv.at[c, core],
            device_id=device(z, 1 - y, cc), device_id_type=MESH,
        )

    def yq_wait(c):
        for cc in range(2):
            pltpu.make_async_remote_copy(
                q_piece(c, cc), qbuf.at[c, 1 - y, z, cc], yq_send.at[c, cc], yq_recv.at[c, cc],
                device_id=device(z, 1 - y, cc), device_id_type=MESH,
            ).wait_recv()

    def pq(c):
        return pltpu.make_async_remote_copy(
            q_piece(c, 1 - core), qbuf.at[c, y, z, core], pq_send.at[c], pq_recv.at[c],
            device_id=device(z, y, 1 - core), device_id_type=MESH,
        )

    def forward(c, d):
        at = zpeer(length - d)
        return pltpu.make_async_remote_copy(
            qbuf.at[c, y, at], qbuf.at[c, y, at], f_send.at[c, d], f_recv.at[c, d],
            device_id=device(z, 1 - y, core), device_id_type=MESH,
        )

    def p_copies(c):
        return tuple(
            pltpu.make_async_remote_copy(
                a.at[c], b.at[c], p_send.at[c, i], p_recv.at[c, i],
                device_id=device(z, 1 - y, core), device_id_type=MESH,
            )
            for i, (a, b) in enumerate(((nsend, narr), (ssend, sarr)))
        )

    def w_copy(c, d, cc):
        return pltpu.make_async_remote_copy(
            wsend.at[c, zpeer(d), cc], warr.at[c, z, core], w_send.at[c, d, cc], w_recv.at[c, d, core],
            device_id=device(zpeer(d), y, cc), device_id_type=MESH,
        )

    def s_copy(d, cc):
        return pltpu.make_async_remote_copy(
            wstat.at[zpeer(d), cc], wsarr.at[z, core],
            w_send.at[CHUNKS, d, cc], w_recv.at[CHUNKS, d, core],
            device_id=device(zpeer(d), y, cc), device_id_type=MESH,
        )

    def wp_copy(c):
        return pltpu.make_async_remote_copy(
            wsend.at[c, z, 1 - core], warr.at[c, z, core], w_send.at[c, 0, 0], w_recv.at[c, 0, 0],
            device_id=device(z, y, 1 - core), device_id_type=MESH,
        )

    def sp_copy():
        return pltpu.make_async_remote_copy(
            wstat.at[z, 1 - core], wsarr.at[z, core],
            w_send.at[CHUNKS, 0, 0], w_recv.at[CHUNKS, 0, 0],
            device_id=device(z, y, 1 - core), device_id_type=MESH,
        )

    for c in range(CHUNKS):
        q_own(c).start()
        for copy in kv_local(c):
            copy.start()
    q_in.wait()
    pl.semaphore_wait(barrier, len(peers))

    for c in range(CHUNKS):
        for d in range(1, length):
            for cc in range(2):
                zq(c, d, cc).start()
        for cc in range(2):
            yq(c, cc).start()
        pq(c).start()
    for copy in self_remote():
        copy.start()
    for c in range(CHUNKS):
        for copy in reversed(kv_remote(c)):
            copy.start()

    for copy in small:
        copy.wait()
    place = chip * docs + lax.broadcasted_iota(jnp.int32, (docs, LANE), 0)
    bias_doc[...] = jnp.where(place < off_ref[0], 0.0, MASKED)
    spot = lax.broadcasted_iota(jnp.int32, (selves, 2 * LANE), 1)
    key_row = chip * selves + lax.broadcasted_iota(jnp.int32, (selves, 2 * LANE), 0)
    inner = spot % side
    row = ((inner // (2 * rows)) * 2 + jnp.where(spot < LANE, y, 1 - y)) * (2 * rows) + inner % (2 * rows)
    bias_self[...] = jnp.where(key_row <= row, 0.0, MASKED)
    for copy in self_remote():
        copy.wait_recv()
    kbuf[docs:, :] = kself[...].astype(jnp.float32).reshape(selves, half_kv).astype(kbuf.dtype)
    vbuf[docs:, :] = vself[...].astype(jnp.float32).reshape(selves, half_kv).astype(kbuf.dtype)
    ones = lax.broadcasted_iota(jnp.int32, (16, docs + LANE), 0) == 0
    ones = jnp.where(ones, 1.0, 0.0).astype(vt.dtype)
    for g in range(HALF_KVH):
        vt[g, HD:, :] = ones

    def turn(c):
        for copy in kv_local(c):
            copy.wait()
        for copy in kv_remote(c):
            copy.wait_recv()
        for g in range(GROUPS):
            cols = slice((c * GROUPS + g) * HD, (c * GROUPS + g + 1) * HD)
            vt[c * GROUPS + g, :HD, :docs] = vbuf[:docs, cols].T
            last = vbuf[docs:, cols].astype(jnp.float32)
            last = jnp.concatenate([last, jnp.zeros((LANE - selves, HD), jnp.float32)], axis=0)
            vt[c * GROUPS + g, :HD, docs:] = last.T.astype(vt.dtype)

    def relay(c):
        for d in range(1, length):
            zq_wait(c, d)
            forward(c, d).start()

    factor = QSCALE ** (-0.5) * LOG2E
    tile = 256

    def attend(c):
        q_own(c).wait()
        pq(c).wait_recv()
        yq_wait(c)
        for d in range(1, length):
            forward(c, d).wait_recv()
        for g in range(GROUPS):
            at = c * GROUPS + g
            cols = slice(at * HD, (at + 1) * HD)
            pieces = []
            for yy in (y, 1 - y):
                for j in range(PER_GROUP):
                    h = g * PER_GROUP + j
                    block = qbuf[c, yy, :, :, :, h * HD : (h + 1) * HD].astype(jnp.float32)
                    pieces.append(block.reshape(side, HD).astype(jnp.bfloat16))
            query = jnp.concatenate(pieces, axis=0)
            top = None
            for start in list(range(0, docs, tile)) + [docs]:
                size = tile if start < docs else selves
                part = lax.dot_general(
                    kbuf[start : start + size, cols], query, (((1,), (1,)), ((), ())),
                    preferred_element_type=jnp.float32,
                )
                if start < docs:
                    mask = bias_doc[start : start + size, :]
                    part = part + jnp.concatenate([mask, mask], axis=1)
                else:
                    part = part + bias_self[...]
                scores[at % 2, start : start + size, :] = part
                most = jnp.max(part.reshape(size // 8, 8, 2 * LANE), axis=0)
                top = most if top is None else jnp.maximum(top, most)
            top = jnp.max(top, axis=0, keepdims=True)
            total = None
            for start in list(range(0, docs, tile)) + [docs]:
                size = tile if start < docs else selves
                part = scores[at % 2, start : start + size, :]
                weights = jnp.exp2((part - top) * factor)
                span = size
                if start == docs:
                    span = LANE
                    weights = jnp.concatenate(
                        [weights, jnp.zeros((LANE - selves, 2 * LANE), jnp.float32)], axis=0
                    )
                got = jnp.dot(
                    vt[at, :, start : start + span], weights.astype(jnp.bfloat16),
                    preferred_element_type=jnp.float32,
                )
                total = got if total is None else total + got
            top = top * factor
            den = total[HD : HD + 1]
            num = total[:HD]
            nkeep[c, g * HD : (g + 1) * HD, :] = num[:, :LANE]
            skeep[c, 3 * g : 3 * g + 1, :] = top[:, :LANE]
            skeep[c, 3 * g + 1 : 3 * g + 2, :] = den[:, :LANE]
            out = num[:, LANE:]
            largest = jnp.maximum(jnp.max(jnp.abs(out), axis=0, keepdims=True), 1e-30)
            nsend[c, g * HD : (g + 1) * HD, :] = encode(out * (WIRE_TOP / largest))
            ssend[c, 3 * g : 3 * g + 1, :] = top[:, LANE:]
            ssend[c, 3 * g + 1 : 3 * g + 2, :] = den[:, LANE:]
            ssend[c, 3 * g + 2 : 3 * g + 3, :] = largest * (1.0 / WIRE_TOP)
        for copy in p_copies(c):
            copy.start()

    def pair_up(c):
        for copy in p_copies(c):
            copy.wait_recv()
        stats = []
        for g in range(GROUPS):
            top_a, top_b = skeep[c, 3 * g : 3 * g + 1, :], sarr[c, 3 * g : 3 * g + 1, :]
            top = jnp.maximum(top_a, top_b)
            fa, fb = jnp.exp2(top_a - top), jnp.exp2(top_b - top)
            den = skeep[c, 3 * g + 1 : 3 * g + 2, :] * fa + sarr[c, 3 * g + 1 : 3 * g + 2, :] * fb
            fb = fb * sarr[c, 3 * g + 2 : 3 * g + 3, :]
            span = slice(g * HD, (g + 1) * HD)
            num = nkeep[c, span, :] * fa + decode(narr[c, span, :]) * fb
            largest = jnp.maximum(jnp.max(jnp.abs(num), axis=0, keepdims=True), 1e-30)
            codes = encode((num * (WIRE_TOP / largest)).T)
            for j in range(PER_GROUP):
                h = g * PER_GROUP + j
                wsend[c, :, :, :, h * HD : (h + 1) * HD] = codes[j * side : (j + 1) * side].reshape(
                    length, 2, rows, HD
                )
            stats += [top, den, largest * (1.0 / WIRE_TOP)]
        stats.append(jnp.zeros((LANE - 3 * GROUPS, LANE), jnp.float32))
        table = jnp.concatenate(stats, axis=0).T
        for j in range(PER_GROUP):
            at = (c * PER_GROUP + j) * STATS
            wstat[:, :, :, at : at + STATS] = table[j * side : (j + 1) * side, :STATS].reshape(
                length, 2, rows, STATS
            )
        for d in range(1, length):
            for cc in range(2):
                if c == CHUNKS - 1:
                    s_copy(d, cc).start()
                w_copy(c, d, cc).start()
        wp_copy(c).start()
        warr[c, z, core] = wsend[c, z, core]
        if c == CHUNKS - 1:
            sp_copy().start()
            wsarr[z, core] = wstat[z, core]

    relay(0)
    turn(0)
    for c in range(CHUNKS):
        if c + 1 < CHUNKS:
            relay(c + 1)
        attend(c)
        if c + 1 < CHUNKS:
            turn(c + 1)
        if c > 0:
            pair_up(c - 1)
    pair_up(CHUNKS - 1)

    mine = me * rows + lax.broadcasted_iota(jnp.int32, (rows, HD), 0)
    live = mine % QL < len_ref[0]

    def w_wait(c, d):
        for cc in range(2):
            pltpu.make_async_remote_copy(
                wsend.at[c, zpeer(d), cc] if c < CHUNKS else wstat.at[zpeer(d), cc],
                warr.at[c, zpeer(length - d), cc] if c < CHUNKS else wsarr.at[zpeer(length - d), cc],
                w_send.at[c, d, cc], w_recv.at[c, d, cc],
                device_id=device(zpeer(d), y, cc), device_id_type=MESH,
            ).wait_recv()

    sp_copy().wait_recv()
    for d in range(1, length):
        w_wait(CHUNKS, d)
    for c in range(CHUNKS):
        wp_copy(c).wait_recv()
        for d in range(1, length):
            w_wait(c, d)
        for cc in range(2):
            for h in range(GROUPS * PER_GROUP):
                g, j = h // PER_GROUP, h % PER_GROUP
                at = (c * PER_GROUP + j) * STATS + 3 * g
                tops = [wsarr[k, cc, :, at : at + 1] for k in range(length)]
                overall = functools.reduce(jnp.maximum, tops)
                shrink = [jnp.exp2(t - overall) for t in tops]
                den = sum(wsarr[k, cc, :, at + 1 : at + 2] * shrink[k] for k in range(length))
                acc = jnp.zeros((rows, HD), jnp.float32)
                for k in range(length):
                    coef = wsarr[k, cc, :, at + 2 : at + 3] * shrink[k] / den
                    acc = acc + decode(warr[c, k, cc, :, h * HD : (h + 1) * HD]) * coef
                to = cc * half_q + c * wide + h * HD
                o_ref[:, to : to + HD] = jnp.where(live, acc, 0.0).astype(o_ref.dtype)

    for copy in self_remote():
        copy.wait_send()
    sp_copy().wait_send()
    for c in range(CHUNKS):
        for copy in kv_remote(c) + p_copies(c):
            copy.wait_send()
        pq(c).wait_send()
        wp_copy(c).wait_send()
        for cc in range(2):
            yq(c, cc).wait_send()
        for d in range(1, length):
            forward(c, d).wait_send()
            for cc in range(2):
                zq(c, d, cc).wait_send()
                w_copy(c, d, cc).wait_send()
    for d in range(1, length):
        for cc in range(2):
            s_copy(d, cc).wait_send()


def encode(x):
    return jnp.round(x).astype(jnp.int32).astype(WIRE)


def decode(x):
    return x.astype(jnp.int32).astype(jnp.float32)


def fused(n, queries, question_keys, question_values, doc_keys, doc_values, lengths, offsets):
    rows = queries.shape[0]
    doc = doc_keys.shape[0]
    if (
        NQ != 1 or n % 4 or n < 8 or rows % 8 or n * rows * PER_GROUP != 2 * LANE
        or doc % LANE or doc > 1024 or n * rows != QL
    ):
        return local(
            queries, question_keys, question_values, doc_keys, doc_values, lengths, offsets
        )
    length = n // 4
    docs, selves = 2 * doc, 2 * rows
    half_kv = HALF_KVH * HD
    wide = GROUPS * PER_GROUP * HD
    vmem = pl.BlockSpec(memory_space=pltpu.VMEM)
    hbm = pl.BlockSpec(memory_space=pl.ANY)
    f32, bf16 = jnp.float32, jnp.bfloat16
    dma = pltpu.SemaphoreType.DMA
    return pl.pallas_call(
        functools.partial(fused_kernel, n),
        out_shape=jax.ShapeDtypeStruct(queries.shape, bf16),
        in_specs=[hbm] * 7,
        out_specs=vmem,
        scratch_shapes=[
            pltpu.VMEM((rows, H * HD), bf16),
            pltpu.VMEM((CHUNKS, 2, length, 2, rows, wide), bf16),
            pltpu.VMEM((2, rows, half_kv), bf16),
            pltpu.VMEM((2, rows, half_kv), bf16),
            pltpu.VMEM((docs + selves, half_kv), bf16),
            pltpu.VMEM((HALF_KVH, HD + 16, docs + LANE), bf16),
            pltpu.VMEM((docs, LANE), f32),
            pltpu.VMEM((selves, 2 * LANE), f32),
            pltpu.VMEM((2, docs + selves, 2 * LANE), f32),
            pltpu.SMEM((1,), jnp.int32),
            pltpu.SMEM((1,), jnp.int32),
            pltpu.VMEM((docs + selves, half_kv), bf16),
            pltpu.VMEM((CHUNKS, GROUPS * HD, LANE), f32),
            pltpu.VMEM((CHUNKS, STATS, LANE), f32),
            pltpu.VMEM((CHUNKS, GROUPS * HD, LANE), WIRE),
            pltpu.VMEM((CHUNKS, STATS, LANE), f32),
            pltpu.VMEM((CHUNKS, GROUPS * HD, LANE), WIRE),
            pltpu.VMEM((CHUNKS, STATS, LANE), f32),
            pltpu.VMEM((CHUNKS, length, 2, rows, wide), WIRE),
            pltpu.VMEM((length, 2, rows, LANE), f32),
            pltpu.VMEM((CHUNKS, length, 2, rows, wide), WIRE),
            pltpu.VMEM((length, 2, rows, LANE), f32),
            dma((CHUNKS + 1,)),
            dma((4,)),
            dma((2, CHUNKS)),
            dma((2, CHUNKS + 1)),
            dma((2, CHUNKS + 1)),
            dma((CHUNKS, length, 2)),
            dma((CHUNKS, length, 2)),
            dma((CHUNKS, 2)),
            dma((CHUNKS, 2)),
            dma((CHUNKS,)),
            dma((CHUNKS,)),
            dma((CHUNKS, length)),
            dma((CHUNKS, length)),
            dma((CHUNKS, 2)),
            dma((CHUNKS, 2)),
            dma((CHUNKS + 1, length, 2)),
            dma((CHUNKS + 1, length, 2)),
        ],
        compiler_params=pltpu.CompilerParams(
            collective_id=0, has_side_effects=True, vmem_limit_bytes=60 * 1024 * 1024
        ),
    )(queries, question_keys, question_values, doc_keys, doc_values, lengths, offsets)


def solution(mesh):
    placed = (
        P(("grp", "seq"), None),
        P(("grp", "seq"), None),
        P(("grp", "seq"), None),
        P(("grp", "seq"), None),
        P(("grp", "seq"), None),
        P("grp"),
        P("grp"),
    )
    return jax.shard_map(
        functools.partial(fused, mesh.shape["seq"]),
        mesh=mesh, in_specs=placed, out_specs=P(("grp", "seq"), None), check_vma=False,
    )
```

time: 41.1 us -> 36.8 us (0.90)
  Pallas kernels: 38.1 us -> 33.8 us
    pallas_call x1, Pallas kernels: 38.1 us -> 33.8 us  [fused(): pl.pallas_call(functools.partial(fused_kernel, n), out_shape=jax.ShapeDty...]
where the time goes in v1:
time: 36.8 us; the launch traced here: 36.6 us
  Pallas kernels  33.8 us (92%)
  local copies, waits for them, and re-layouts  1.47 us (4%)
  between operations  1.3 us (4%)
    pallas_call x1, Pallas kernels, fused(): pl.pallas_call(functools.partial(fused_kernel, n), out_shape=jax.ShapeDty...  33.8 us
    unnamed x1, local copies, waits for them, and re-layouts  1.47 us

profile of v1, /device:TPU:0, one launch (start us, length us, event | category | flops | bytes accessed | tf_op | source)
XLA Modules:
  0.0 36.6 jit_solution(566363700204538312)
XLA Ops:
  1.3 33.8 %shard_map.73 = bf16[8,4096]{1,0:T(8,128)(2,1)} custom-call(bf16[8,4096]{1,0:T(8,128)(2,1)} %q_hbm.1, bf16[8,2048]{1,0:T(8,128)(2,1)} %qk_hbm.1, bf16[8,2048]{1,0:T(8,128)(2,1)} %qv_hbm.1, bf16[512,2048]{1,0:T(8,128)(2,1)} %k_hbm.1, bf16[512,2048]{1,0:T(8,128)(2,1)} %v_hbm.1, s32[1]{0:T(128)S(6)} %copy.9.len_hbm, s32[1]{0:T(128)S(6)} %copy.10.off_hbm), custom_call_target="tpu_custom_call" | custom-call | tf_op jit(solution)/shard_map/pallas_call | solution.py:541
  35.1 1.5 %copy.11 = bf16[8,4096]{1,0:T(8,128)(2,1)} copy(bf16[8,4096]{1,0:T(8,128)(2,1)} %shard_map.73) | data formatting | bytes 131072

commit v2 on v1

v2 whole, which is shorter than its diff:
```python
import functools
import math

import jax
import jax.numpy as jnp
from jax import lax
from jax.experimental import pallas as pl
from jax.experimental.pallas import tpu as pltpu
from jax.sharding import PartitionSpec as P

H = 32
KVH = 16
HD = 128
QSCALE = 144
QL = 128
NQ = 1


MASKED = -1e30


def row_tables(start, count, lengths, offsets):
    rows = start + jnp.arange(count, dtype=jnp.int32)
    question = rows // QL
    position = rows % QL
    owner_table = question[:, None] == jnp.arange(NQ, dtype=jnp.int32)[None, :]
    row_length = jnp.sum(jnp.where(owner_table, lengths[None, :], 0), axis=1)
    row_offset = jnp.sum(jnp.where(owner_table, offsets[None, :], 0), axis=1)
    return (question, position, position < row_length, row_offset)


def local(queries, question_keys, question_values, doc_keys, doc_values, lengths, offsets):
    rows_local = queries.shape[0]
    doc_local = doc_keys.shape[0]
    device_count = lax.axis_size("seq")
    device_index = lax.axis_index("seq")
    total_rows = rows_local * device_count
    per_group = H // KVH
    factor_q = QSCALE ** (-0.5)
    key_doc = doc_keys.reshape(doc_local, KVH, HD)
    value_doc = doc_values.reshape(doc_local, KVH, HD)
    key_self = question_keys.reshape(rows_local, KVH, HD)
    value_self = question_values.reshape(rows_local, KVH, HD)
    doc_places = device_index * doc_local + jnp.arange(doc_local, dtype=jnp.int32)
    self_rows = device_index * rows_local + jnp.arange(rows_local, dtype=jnp.int32)
    whole = lax.all_gather(queries, "seq", axis=0, tiled=True)
    block_rows = math.gcd(total_rows, 512)
    block_count = total_rows // block_rows

    def one_block(start):
        piece = whole.reshape(block_rows, KVH, per_group, HD)
        question, position, live_rows, row_offset = row_tables(start, block_rows, lengths, offsets)
        mask_doc = live_rows[:, None] & (doc_places[None, :] < row_offset[:, None])
        mask_self = (
            live_rows[:, None]
            & (self_rows[None, :] // QL == question[:, None])
            & (self_rows[None, :] % QL <= position[:, None])
        )
        mask_doc = mask_doc[:, None, None, :]
        mask_self = mask_self[:, None, None, :]
        scores_doc = (
            jnp.einsum("rgjd,kgd->rgjk", piece, key_doc, preferred_element_type=jnp.float32)
            * factor_q
        )
        scores_self = (
            jnp.einsum("rgjd,kgd->rgjk", piece, key_self, preferred_element_type=jnp.float32)
            * factor_q
        )
        scores_doc = jnp.where(mask_doc, scores_doc, MASKED)
        scores_self = jnp.where(mask_self, scores_self, MASKED)
        block_top = jnp.maximum(jnp.max(scores_doc, axis=-1), jnp.max(scores_self, axis=-1))
        weights_doc = jnp.where(mask_doc, jnp.exp(scores_doc - block_top[..., None]), 0.0).astype(
            jnp.bfloat16
        )
        weights_self = jnp.where(
            mask_self, jnp.exp(scores_self - block_top[..., None]), 0.0
        ).astype(jnp.bfloat16)
        block_den = jnp.sum(weights_doc.astype(jnp.float32), axis=-1) + jnp.sum(
            weights_self.astype(jnp.float32), axis=-1
        )
        block_num = jnp.einsum(
            "rgjk,kgd->rgjd", weights_doc, value_doc, preferred_element_type=jnp.float32
        )
        block_num = block_num + jnp.einsum(
            "rgjk,kgd->rgjd", weights_self, value_self, preferred_element_type=jnp.float32
        )
        return (
            block_num.reshape(block_rows, H * HD),
            block_top.reshape(block_rows, H),
            block_den.reshape(block_rows, H),
        )

    starts = jnp.arange(block_count, dtype=jnp.int32) * block_rows
    numer, row_top, denom = lax.map(one_block, starts)
    numer = numer.reshape(total_rows, H * HD)
    row_top = row_top.reshape(total_rows, H)
    denom = denom.reshape(total_rows, H)
    got_num, got_top, got_den = (
        lax.all_to_all(numer[None], "seq", split_axis=1, concat_axis=0, tiled=True),
        lax.all_to_all(row_top[None], "seq", split_axis=1, concat_axis=0, tiled=True),
        lax.all_to_all(denom[None], "seq", split_axis=1, concat_axis=0, tiled=True),
    )
    overall = jnp.max(got_top, axis=0)
    rescale = jnp.exp(got_top - overall[None])
    total_num = jnp.sum(
        got_num.reshape(device_count, rows_local, H, HD) * rescale[:, :, :, None], axis=0
    )
    total_den = jnp.sum(got_den * rescale, axis=0)
    question, position, live_rows, row_offset = row_tables(
        device_index * rows_local, rows_local, lengths, offsets
    )
    safe_den = jnp.where(live_rows[:, None], total_den, 1.0)
    result = (total_num / safe_den[:, :, None]).reshape(rows_local, H * HD)
    return jnp.where(live_rows[:, None], result, 0.0).astype(jnp.bfloat16)


MESH = pl.DeviceIdType.MESH
LANE = 128
CHUNKS = 4
PIECES = 2
LOG2E = math.log2(math.e)
WIRE = jnp.int16
WIRE_TOP = 32767.0
HALF_KVH = KVH // 2
PER_GROUP = H // KVH
GROUPS = HALF_KVH // CHUNKS
STATS = 8


def fused_kernel(
    n, q_hbm, qk_hbm, qv_hbm, k_hbm, v_hbm, len_ref, off_ref, o_ref,
    qown, qbuf, kself, vself, kbuf, vt, bias_doc, bias_self, scores, vbuf,
    nkeep, skeep, nsend, narr, wsend, warr, osend,
    q_sem, in_sem, kv_sem, kv_send, kv_recv,
    zq_send, zq_recv, yq_send, yq_recv, pq_send, pq_recv, f_send, f_recv,
    p_send, p_recv, w_send, w_recv, o_send, o_recv,
):
    length = n // 4
    rows = q_hbm.shape[0]
    doc = k_hbm.shape[0]
    docs = 2 * doc
    selves = 2 * rows
    half_kv = HALF_KVH * HD
    half_q = half_kv * PER_GROUP
    kv_wide = GROUPS * HD
    wide = kv_wide * PER_GROUP
    q_wide = half_q // PIECES
    side = length * 2 * rows
    me = lax.axis_index("seq")
    core = lax.rem(me, 2)
    chip = me // 2
    y = lax.rem(chip, 2)
    z = chip // 2
    others = (z + 1 - 2 * lax.rem(z, 2), 2 - z // 2, 3 - 3 * (z // 2))

    def device(zz, yy, cc):
        return {"seq": (zz * 2 + yy) * 2 + cc}

    barrier = pltpu.get_barrier_semaphore()
    peers = [device(zz, y, cc) for zz in others for cc in range(2)]
    peers += [device(z, 1 - y, cc) for cc in range(2)] + [device(z, y, 1 - core)]
    for peer in peers:
        pl.semaphore_signal(barrier, inc=1, device_id=peer, device_id_type=MESH)

    q_in = pltpu.make_async_copy(q_hbm, qown, q_sem.at[PIECES])
    q_in.start()
    small = [
        pltpu.make_async_copy(qk_hbm.at[:, pl.ds(core * half_kv, half_kv)], kself.at[core], in_sem.at[0]),
        pltpu.make_async_copy(qv_hbm.at[:, pl.ds(core * half_kv, half_kv)], vself.at[core], in_sem.at[1]),
    ]
    for copy in small:
        copy.start()

    def q_own(c):
        return pltpu.make_async_copy(
            q_hbm.at[:, pl.ds(core * half_q + c * q_wide, q_wide)], qbuf.at[c, y, z, core], q_sem.at[c]
        )

    def kv_local(c):
        cols = pl.ds(core * half_kv + c * kv_wide, kv_wide)
        at = pl.ds(core * doc, doc)
        to = pl.ds(c * kv_wide, kv_wide)
        return (
            pltpu.make_async_copy(k_hbm.at[:, cols], kbuf.at[at, to], kv_sem.at[0, c]),
            pltpu.make_async_copy(v_hbm.at[:, cols], vbuf.at[at, to], kv_sem.at[1, c]),
        )

    def kv_remote(c):
        cols = pl.ds((1 - core) * half_kv + c * kv_wide, kv_wide)
        at = pl.ds(core * doc, doc)
        to = pl.ds(c * kv_wide, kv_wide)
        return tuple(
            pltpu.make_async_remote_copy(
                a.at[:, cols], b.at[at, to], kv_send.at[i, c], kv_recv.at[i, c],
                device_id=device(z, y, 1 - core), device_id_type=MESH,
            )
            for i, (a, b) in enumerate(((k_hbm, kbuf), (v_hbm, vbuf)))
        )

    def self_remote():
        cols = pl.ds((1 - core) * half_kv, half_kv)
        return tuple(
            pltpu.make_async_remote_copy(
                a.at[:, cols], b.at[core], kv_send.at[i, CHUNKS], kv_recv.at[i, CHUNKS],
                device_id=device(z, y, 1 - core), device_id_type=MESH,
            )
            for i, (a, b) in enumerate(((qk_hbm, kself), (qv_hbm, vself)))
        )

    def q_piece(c, cc):
        return qown.at[:, pl.ds(cc * half_q + c * q_wide, q_wide)]

    def zq(c, zz, cc):
        return pltpu.make_async_remote_copy(
            q_piece(c, cc), qbuf.at[c, y, z, core], zq_send.at[c, zz, cc], zq_recv.at[c, z, core],
            device_id=device(zz, y, cc), device_id_type=MESH,
        )

    def zq_wait(c, zz):
        for cc in range(2):
            pltpu.make_async_remote_copy(
                q_piece(c, cc), qbuf.at[c, y, zz, cc], zq_send.at[c, zz, cc], zq_recv.at[c, zz, cc],
                device_id=device(zz, y, cc), device_id_type=MESH,
            ).wait_recv()

    def yq(c, cc):
        return pltpu.make_async_remote_copy(
            q_piece(c, cc), qbuf.at[c, y, z, core], yq_send.at[c, cc], yq_recv.at[c, core],
            device_id=device(z, 1 - y, cc), device_id_type=MESH,
        )

    def yq_wait(c):
        for cc in range(2):
            pltpu.make_async_remote_copy(
                q_piece(c, cc), qbuf.at[c, 1 - y, z, cc], yq_send.at[c, cc], yq_recv.at[c, cc],
                device_id=device(z, 1 - y, cc), device_id_type=MESH,
            ).wait_recv()

    def pq(c):
        return pltpu.make_async_remote_copy(
            q_piece(c, 1 - core), qbuf.at[c, y, z, core], pq_send.at[c], pq_recv.at[c],
            device_id=device(z, y, 1 - core), device_id_type=MESH,
        )

    def forward(c, zz):
        return pltpu.make_async_remote_copy(
            qbuf.at[c, y, zz], qbuf.at[c, y, zz], f_send.at[c, zz], f_recv.at[c, zz],
            device_id=device(z, 1 - y, core), device_id_type=MESH,
        )

    def p_copy(c):
        return pltpu.make_async_remote_copy(
            nsend.at[c], narr.at[c], p_send.at[c], p_recv.at[c],
            device_id=device(z, 1 - y, core), device_id_type=MESH,
        )

    def w_copy(c, zz):
        return pltpu.make_async_remote_copy(
            wsend.at[c, zz], warr.at[c, z], w_send.at[c, zz], w_recv.at[c, z],
            device_id=device(zz, y, core), device_id_type=MESH,
        )

    def w_wait(c, zz):
        pltpu.make_async_remote_copy(
            wsend.at[c, zz], warr.at[c, zz], w_send.at[c, zz], w_recv.at[c, zz],
            device_id=device(zz, y, core), device_id_type=MESH,
        ).wait_recv()

    def o_copy(c):
        return pltpu.make_async_remote_copy(
            osend.at[c], o_ref.at[:, pl.ds(core * half_q + c * wide, wide)], o_send.at[c], o_recv.at[c],
            device_id=device(z, y, 1 - core), device_id_type=MESH,
        )

    for c in range(PIECES):
        q_own(c).start()
    for c in range(CHUNKS):
        for copy in reversed(kv_local(c)):
            copy.start()
    with jax.named_scope("enter"):
        q_in.wait()
        pl.semaphore_wait(barrier, len(peers))

    for c in range(PIECES):
        for zz in reversed(others):
            for cc in range(2):
                zq(c, zz, cc).start()
        for cc in range(2):
            yq(c, cc).start()
        pq(c).start()
        if c == 0:
            for copy in self_remote():
                copy.start()
    for c in range(CHUNKS):
        for copy in reversed(kv_remote(c)):
            copy.start()

    for copy in small:
        copy.wait()
    place = chip * docs + lax.broadcasted_iota(jnp.int32, (docs, LANE), 0)
    bias_doc[...] = jnp.where(place < off_ref[0], 0.0, MASKED)
    spot = lax.broadcasted_iota(jnp.int32, (selves, 2 * LANE), 1)
    key_row = chip * selves + lax.broadcasted_iota(jnp.int32, (selves, 2 * LANE), 0)
    inner = spot % side
    row = ((inner // (2 * rows)) * 2 + jnp.where(spot < LANE, y, 1 - y)) * (2 * rows) + inner % (2 * rows)
    bias_self[...] = jnp.where(key_row <= row, 0.0, MASKED)
    ones = lax.broadcasted_iota(jnp.int32, (16, docs + LANE), 0) == 0
    ones = jnp.where(ones, 1.0, 0.0).astype(vt.dtype)
    for g in range(HALF_KVH):
        vt[g, HD:, :] = ones
    for copy in self_remote():
        copy.wait_recv()
    kbuf[docs:, :] = kself[...].astype(jnp.float32).reshape(selves, half_kv).astype(kbuf.dtype)
    vbuf[docs:, :] = vself[...].astype(jnp.float32).reshape(selves, half_kv).astype(kbuf.dtype)

    def turn(c):
        with jax.named_scope("kv"):
            for copy in kv_local(c):
                copy.wait()
            for copy in kv_remote(c):
                copy.wait_recv()
        for g in range(GROUPS):
            cols = slice((c * GROUPS + g) * HD, (c * GROUPS + g + 1) * HD)
            vt[c * GROUPS + g, :HD, :docs] = vbuf[:docs, cols].T
            last = vbuf[docs:, cols].astype(jnp.float32)
            last = jnp.concatenate([last, jnp.zeros((LANE - selves, HD), jnp.float32)], axis=0)
            vt[c * GROUPS + g, :HD, docs:] = last.T.astype(vt.dtype)

    def relay(c):
        for zz in others:
            zq_wait(c, zz)
            forward(c, zz).start()

    factor = QSCALE ** (-0.5) * LOG2E
    tile = 256
    per_piece = CHUNKS // PIECES

    def attend(c):
        piece = c // per_piece
        if c % per_piece == 0:
            with jax.named_scope("queries"):
                q_own(piece).wait()
                pq(piece).wait_recv()
                yq_wait(piece)
                for zz in others:
                    forward(piece, zz).wait_recv()
        for g in range(GROUPS):
            at = c * GROUPS + g
            cols = slice(at * HD, (at + 1) * HD)
            pieces = []
            for yy in (y, 1 - y):
                for j in range(PER_GROUP):
                    h = ((c % per_piece) * GROUPS + g) * PER_GROUP + j
                    block = qbuf[piece, yy, :, :, :, h * HD : (h + 1) * HD].astype(jnp.float32)
                    pieces.append(block.reshape(side, HD).astype(jnp.bfloat16))
            query = jnp.concatenate(pieces, axis=0)
            top = None
            for start in list(range(0, docs, tile)) + [docs]:
                size = tile if start < docs else selves
                part = lax.dot_general(
                    kbuf[start : start + size, cols], query, (((1,), (1,)), ((), ())),
                    preferred_element_type=jnp.float32,
                )
                if start < docs:
                    mask = bias_doc[start : start + size, :]
                    part = part + jnp.concatenate([mask, mask], axis=1)
                else:
                    part = part + bias_self[...]
                scores[at % 2, start : start + size, :] = part
                most = jnp.max(part.reshape(size // 8, 8, 2 * LANE), axis=0)
                top = most if top is None else jnp.maximum(top, most)
            top = jnp.max(top, axis=0, keepdims=True)
            total = None
            for start in list(range(0, docs, tile)) + [docs]:
                size = tile if start < docs else selves
                part = scores[at % 2, start : start + size, :]
                weights = jnp.exp2((part - top) * factor)
                span = size
                if start == docs:
                    span = LANE
                    weights = jnp.concatenate(
                        [weights, jnp.zeros((LANE - selves, 2 * LANE), jnp.float32)], axis=0
                    )
                got = jnp.dot(
                    vt[at, :, start : start + span], weights.astype(jnp.bfloat16),
                    preferred_element_type=jnp.float32,
                )
                total = got if total is None else total + got
            top = top * factor
            den = total[HD : HD + 1]
            num = total[:HD]
            nkeep[c, g * HD : (g + 1) * HD, :] = num[:, :LANE]
            skeep[c, 2 * g : 2 * g + 1, :] = top[:, :LANE]
            skeep[c, 2 * g + 1 : 2 * g + 2, :] = den[:, :LANE]
            out = num[:, LANE:]
            largest = jnp.maximum(jnp.max(jnp.abs(out), axis=0, keepdims=True), 1e-30)
            nsend[c, g * HD : (g + 1) * HD, :] = encode(out * (WIRE_TOP / largest))
            skeep[c, 4 + g : 5 + g, :] = top[:, LANE:] + log2(den[:, LANE:])
            skeep[c, 6 + g : 7 + g, :] = top[:, LANE:] + log2(largest)
        logs = split(skeep[c, 4:8, :])
        logs = jnp.concatenate([logs, jnp.zeros((8, LANE), jnp.float32)], axis=0)
        nsend[c, GROUPS * HD :, :] = encode(logs)
        p_copy(c).start()

    def pair_up(c):
        with jax.named_scope("pair"):
            p_copy(c).wait_recv()
        logs = decode(narr[c, GROUPS * HD :, :])
        logs = logs[:4] * COARSE + logs[4:8] * FINE
        mass, span = [], []
        for g in range(GROUPS):
            top_a, den_a = skeep[c, 2 * g : 2 * g + 1, :], skeep[c, 2 * g + 1 : 2 * g + 2, :]
            mass_b, span_b = logs[g : g + 1], logs[2 + g : 3 + g]
            top = jnp.maximum(top_a, mass_b)
            fa = jnp.exp2(top_a - top)
            den = den_a * fa + jnp.exp2(mass_b - top)
            fb = jnp.exp2(span_b - top) * (1.0 / WIRE_TOP)
            at = slice(g * HD, (g + 1) * HD)
            num = nkeep[c, at, :] * fa + decode(narr[c, at, :]) * fb
            largest = jnp.maximum(jnp.max(jnp.abs(num), axis=0, keepdims=True), 1e-30)
            codes = encode((num * (WIRE_TOP / largest)).T)
            for j in range(PER_GROUP):
                h = g * PER_GROUP + j
                wsend[c, :, :, h * HD : (h + 1) * HD] = codes[j * side : (j + 1) * side].reshape(
                    length, 2 * rows, HD
                )
            mass.append(top + log2(den))
            span.append(top + log2(largest))
        table = split(jnp.concatenate(mass + span, axis=0))
        table = jnp.concatenate([table, jnp.zeros((LANE - 8, LANE), jnp.float32)], axis=0)
        table = encode(table.T)
        for j in range(PER_GROUP):
            wsend[c, :, :, wide + 8 * j : wide + 8 * j + 8] = table[j * side : (j + 1) * side, :8].reshape(
                length, 2 * rows, 8
            )
        for zz in reversed(others):
            w_copy(c, zz).start()
        warr[c, z] = wsend[c, z]

    def finish(c):
        with jax.named_scope("parts"):
            for zz in others:
                w_wait(c, zz)
        logs = []
        for k in range(length):
            block = decode(warr[c, k, :, wide:])
            logs.append(block * COARSE + pltpu.roll(block, LANE - 4, 1) * FINE)
        most = functools.reduce(jnp.maximum, logs)
        den = sum(jnp.exp2(x - most) for x in logs)
        most, den = pltpu.roll(most, 2, 1), pltpu.roll(den, 2, 1)
        share = 1.0 / (den * WIRE_TOP)
        coefs = [jnp.exp2(x - most) * share for x in logs]
        mine = chip * selves + lax.broadcasted_iota(jnp.int32, (selves, HD), 0)
        live = mine < len_ref[0]
        for g in range(GROUPS):
            for j in range(PER_GROUP):
                h = g * PER_GROUP + j
                at = 8 * j + 2 + g
                acc = None
                for k in range(length):
                    term = decode(warr[c, k, :, h * HD : (h + 1) * HD]) * coefs[k][:, at : at + 1]
                    acc = term if acc is None else acc + term
                acc = jnp.where(live, acc, 0.0)
                kept = jnp.where(core == 0, acc[:rows], acc[rows:])
                sent = jnp.where(core == 0, acc[rows:], acc[:rows])
                to = pl.multiple_of(core * half_q + c * wide + h * HD, HD)
                o_ref[:, pl.ds(to, HD)] = kept.astype(o_ref.dtype)
                osend[c, :, h * HD : (h + 1) * HD] = sent.astype(o_ref.dtype)
        o_copy(c).start()

    def drain():
        for copy in self_remote():
            copy.wait_send()
        for c in range(CHUNKS):
            for copy in kv_remote(c):
                copy.wait_send()
        for c in range(PIECES):
            pq(c).wait_send()
            for cc in range(2):
                yq(c, cc).wait_send()
            for zz in others:
                forward(c, zz).wait_send()
                for cc in range(2):
                    zq(c, zz, cc).wait_send()
        for c in range(CHUNKS):
            p_copy(c).wait_send()

    def run(name, step, c):
        with jax.named_scope(f"{name}#c={c}"):
            step(c)

    run("relay", relay, 0)
    run("turn", turn, 0)
    run("turn", turn, 1)
    run("relay", relay, 1)
    for c in range(CHUNKS):
        run("attend", attend, c)
        if c + 2 < CHUNKS:
            run("turn", turn, c + 2)
        if c > 0:
            run("pair_up", pair_up, c - 1)
    run("pair_up", pair_up, CHUNKS - 1)
    with jax.named_scope("drain"):
        drain()
    for c in range(CHUNKS):
        run("finish", finish, c)
    with jax.named_scope("last"):
        for c in range(CHUNKS):
            for zz in others:
                w_copy(c, zz).wait_send()
            o_copy(c).wait_send()
        for c in range(CHUNKS):
            pltpu.make_async_remote_copy(
                osend.at[c], o_ref.at[:, pl.ds((1 - core) * half_q + c * wide, wide)],
                o_send.at[c], o_recv.at[c], device_id=device(z, y, 1 - core), device_id_type=MESH,
            ).wait_recv()


COARSE = 2.0 ** -5
FINE = 2.0 ** -20


def split(x):
    x = jnp.maximum(x, -1000.0)
    high = jnp.round(x * (1.0 / COARSE))
    return jnp.concatenate([high, (x - high * COARSE) * (1.0 / FINE)], axis=0)


def log2(x):
    return jnp.log(x) * LOG2E


def encode(x):
    return jnp.round(x).astype(jnp.int32).astype(WIRE)


def decode(x):
    return x.astype(jnp.int32).astype(jnp.float32)


def fused(n, queries, question_keys, question_values, doc_keys, doc_values, lengths, offsets):
    rows = queries.shape[0]
    doc = doc_keys.shape[0]
    if (
        NQ != 1 or n != 16 or rows % 8 or n * rows * PER_GROUP != 2 * LANE
        or doc % LANE or doc > 1024 or n * rows != QL
    ):
        return local(
            queries, question_keys, question_values, doc_keys, doc_values, lengths, offsets
        )
    operands = (queries, question_keys, question_values, doc_keys, doc_values)
    length = n // 4
    docs, selves = 2 * doc, 2 * rows
    half_kv = HALF_KVH * HD
    wide = GROUPS * PER_GROUP * HD
    q_wide = half_kv * PER_GROUP // PIECES
    vmem = pl.BlockSpec(memory_space=pltpu.VMEM)
    hbm = pl.BlockSpec(memory_space=pltpu.HBM)
    smem = pl.BlockSpec(memory_space=pltpu.SMEM)
    f32, bf16 = jnp.float32, jnp.bfloat16
    dma = pltpu.SemaphoreType.DMA
    return pl.pallas_call(
        functools.partial(fused_kernel, n),
        out_shape=jax.ShapeDtypeStruct(queries.shape, bf16),
        in_specs=[hbm] * 5 + [smem] * 2,
        out_specs=vmem,
        scratch_shapes=[
            pltpu.VMEM((rows, H * HD), bf16),
            pltpu.VMEM((PIECES, 2, length, 2, rows, q_wide), bf16),
            pltpu.VMEM((2, rows, half_kv), bf16),
            pltpu.VMEM((2, rows, half_kv), bf16),
            pltpu.VMEM((docs + selves, half_kv), bf16),
            pltpu.VMEM((HALF_KVH, HD + 16, docs + LANE), bf16),
            pltpu.VMEM((docs, LANE), f32),
            pltpu.VMEM((selves, 2 * LANE), f32),
            pltpu.VMEM((2, docs + selves, 2 * LANE), f32),
            pltpu.VMEM((docs + selves, half_kv), bf16),
            pltpu.VMEM((CHUNKS, GROUPS * HD, LANE), f32),
            pltpu.VMEM((CHUNKS, STATS, LANE), f32),
            pltpu.VMEM((CHUNKS, GROUPS * HD + 16, LANE), WIRE),
            pltpu.VMEM((CHUNKS, GROUPS * HD + 16, LANE), WIRE),
            pltpu.VMEM((CHUNKS, length, 2 * rows, wide + LANE), WIRE),
            pltpu.VMEM((CHUNKS, length, 2 * rows, wide + LANE), WIRE),
            pltpu.VMEM((CHUNKS, rows, wide), bf16),
            dma((PIECES + 1,)),
            dma((2,)),
            dma((2, CHUNKS)),
            dma((2, CHUNKS + 1)),
            dma((2, CHUNKS + 1)),
            dma((PIECES, length, 2)),
            dma((PIECES, length, 2)),
            dma((PIECES, 2)),
            dma((PIECES, 2)),
            dma((PIECES,)),
            dma((PIECES,)),
            dma((PIECES, length)),
            dma((PIECES, length)),
            dma((CHUNKS,)),
            dma((CHUNKS,)),
            dma((CHUNKS, length)),
            dma((CHUNKS, length)),
            dma((CHUNKS,)),
            dma((CHUNKS,)),
        ],
        compiler_params=pltpu.CompilerParams(
            collective_id=0, has_side_effects=True, vmem_limit_bytes=24 * 1024 * 1024
        ),
    )(*(pltpu.with_memory_space_constraint(x, pltpu.HBM) for x in operands), lengths, offsets)


def solution(mesh):
    placed = (
        P(("grp", "seq"), None),
        P(("grp", "seq"), None),
        P(("grp", "seq"), None),
        P(("grp", "seq"), None),
        P(("grp", "seq"), None),
        P("grp"),
        P("grp"),
    )
    return jax.shard_map(
        functools.partial(fused, mesh.shape["seq"]),
        mesh=mesh, in_specs=placed, out_specs=P(("grp", "seq"), None), check_vma=False,
    )
```

time: 36.8 us -> 34.4 us (0.935)
  Pallas kernels: 33.8 us -> 32.3 us
  local copies, waits for them, and re-layouts: 1.47 us -> 0.63 us
    pallas_call x1, Pallas kernels: 33.8 us -> 32.3 us  [fused(): pl.pallas_call(functools.partial(fused_kernel, n), out_shape=jax.ShapeDty...]
    unnamed x1, local copies, waits for them, and re-layouts: 1.47 us -> 0.63 us
where the time goes in v2:
time: 34.4 us; the launch traced here: 34.2 us
  Pallas kernels  32.3 us (94%)
  between operations  1.3 us (4%)
  local copies, waits for them, and re-layouts  0.63 us (2%)
    pallas_call x1, Pallas kernels, fused(): pl.pallas_call(functools.partial(fused_kernel, n), out_shape=jax.ShapeDty...  32.3 us

profile of v2, /device:TPU:0, one launch (start us, length us, event | category | flops | bytes accessed | tf_op | source)
XLA Modules:
  0.0 34.2 jit_solution(11888795339547010424)
XLA Ops:
  1.3 32.3 %shard_map.73 = bf16[8,4096]{1,0:T(8,128)(2,1)S(1)} custom-call(bf16[8,4096]{1,0:T(8,128)(2,1)} %q_hbm.1, bf16[8,2048]{1,0:T(8,128)(2,1)} %qk_hbm.1, bf16[8,2048]{1,0:T(8,128)(2,1)} %qv_hbm.1, bf16[512,2048]{1,0:T(8,128)(2,1)} %k_hbm.1, bf16[512,2048]{1,0:T(8,128)(2,1)} %v_hbm.1, s32[1]{0:T(128)S(6)} %copy.9.len_ref, s32[1]{0:T(128)S(6)} %copy.10.off_ref), custom_call_target="tpu_custom_call" | custom-call | tf_op jit(solution)/shard_map/pallas_call | solution.py:562
  33.6 0.6 %copy.11 = bf16[8,4096]{1,0:T(8,128)(2,1)} copy(bf16[8,4096]{1,0:T(8,128)(2,1)S(1)} %shard_map.73) | data formatting | bytes 131072

commit v3 on v2

--- a/solution.py
+++ b/solution.py
@@ -117,7 +117,8 @@
 MESH = pl.DeviceIdType.MESH
 LANE = 128
 CHUNKS = 4
-PIECES = 2
+PIECES = ((0, 1), (1, 4))
+WHOLE = (0, 4)
 LOG2E = math.log2(math.e)
 WIRE = jnp.int16
 WIRE_TOP = 32767.0
@@ -125,14 +126,16 @@
 PER_GROUP = H // KVH
 GROUPS = HALF_KVH // CHUNKS
 STATS = 8
+QK_TILE = 256
+AHEAD = True
 
 
 def fused_kernel(
     n, q_hbm, qk_hbm, qv_hbm, k_hbm, v_hbm, len_ref, off_ref, o_ref,
-    qown, qbuf, kself, vself, kbuf, vt, bias_doc, bias_self, scores, vbuf,
+    qown, qbuf, kself, vself, kbuf, vt, key_mask, row_mask, scores, probs, vbuf,
     nkeep, skeep, nsend, narr, wsend, warr, osend,
     q_sem, in_sem, kv_sem, kv_send, kv_recv,
-    zq_send, zq_recv, yq_send, yq_recv, pq_send, pq_recv, f_send, f_recv,
+    zq_send, zq_recv, yq_send, yq_recv, pq_recv, f_send, f_recv, far,
     p_send, p_recv, w_send, w_recv, o_send, o_recv,
 ):
     length = n // 4
@@ -144,7 +147,6 @@
     half_q = half_kv * PER_GROUP
     kv_wide = GROUPS * HD
     wide = kv_wide * PER_GROUP
-    q_wide = half_q // PIECES
     side = length * 2 * rows
     me = lax.axis_index("seq")
     core = lax.rem(me, 2)
@@ -156,13 +158,21 @@
     def device(zz, yy, cc):
         return {"seq": (zz * 2 + yy) * 2 + cc}
 
+    middle = (lax.rem(z, length - 1) + 1) // 2
+    across = 1 + lax.rem(z, 2)
+    near = others[0]
     barrier = pltpu.get_barrier_semaphore()
-    peers = [device(zz, y, cc) for zz in others for cc in range(2)]
-    peers += [device(z, 1 - y, cc) for cc in range(2)] + [device(z, y, 1 - core)]
+    peers = [device(z, y, 1 - core)] + [device(z, 1 - y, cc) for cc in range(2)]
+    peers += [device(near, y, cc) for cc in range(2)]
     for peer in peers:
         pl.semaphore_signal(barrier, inc=1, device_id=peer, device_id_type=MESH)
 
-    q_in = pltpu.make_async_copy(q_hbm, qown, q_sem.at[PIECES])
+    @pl.when(middle == 1)
+    def greet():
+        for cc in range(2):
+            pl.semaphore_signal(barrier, inc=1, device_id=device(across, y, cc), device_id_type=MESH)
+
+    q_in = pltpu.make_async_copy(q_hbm, qown, q_sem.at[1])
     q_in.start()
     small = [
         pltpu.make_async_copy(qk_hbm.at[:, pl.ds(core * half_kv, half_kv)], kself.at[core], in_sem.at[0]),
@@ -171,10 +181,10 @@
     for copy in small:
         copy.start()
 
-    def q_own(c):
-        return pltpu.make_async_copy(
-            q_hbm.at[:, pl.ds(core * half_q + c * q_wide, q_wide)], qbuf.at[c, y, z, core], q_sem.at[c]
-        )
+    def part(piece):
+        return pl.ds(piece[0] * wide, (piece[1] - piece[0]) * wide)
+
+    q_own = pltpu.make_async_copy(q_hbm.at[:, pl.ds(core * half_q, half_q)], qbuf.at[y, z, core], q_sem.at[0])
 
     def kv_local(c):
         cols = pl.ds(core * half_kv + c * kv_wide, kv_wide)
@@ -207,44 +217,39 @@
             for i, (a, b) in enumerate(((qk_hbm, kself), (qv_hbm, vself)))
         )
 
-    def q_piece(c, cc):
-        return qown.at[:, pl.ds(cc * half_q + c * q_wide, q_wide)]
-
-    def zq(c, zz, cc):
+    def q_copy(where, i, piece, send_sem, recv_sem):
+        zz, yy, cc = where
         return pltpu.make_async_remote_copy(
-            q_piece(c, cc), qbuf.at[c, y, z, core], zq_send.at[c, zz, cc], zq_recv.at[c, z, core],
-            device_id=device(zz, y, cc), device_id_type=MESH,
-        )
-
-    def zq_wait(c, zz):
-        for cc in range(2):
-            pltpu.make_async_remote_copy(
-                q_piece(c, cc), qbuf.at[c, y, zz, cc], zq_send.at[c, zz, cc], zq_recv.at[c, zz, cc],
-                device_id=device(zz, y, cc), device_id_type=MESH,
-            ).wait_recv()
-
-    def yq(c, cc):
+            qown.at[:, pl.ds(cc * half_q + piece[0] * wide, (piece[1] - piece[0]) * wide)],
+            qbuf.at[y, z, core, :, part(piece)], send_sem.at[i, zz, cc], recv_sem.at[i, z, core],
+            device_id=device(zz, yy, cc), device_id_type=MESH,
+        )
+
+    def q_wait(where, i, piece, send_sem, recv_sem):
+        zz, yy, cc = where
+        pltpu.make_async_remote_copy(
+            qown.at[:, part(piece)], qbuf.at[yy, zz, cc, :, part(piece)],
+            send_sem.at[i, zz, cc], recv_sem.at[i, zz, cc],
+            device_id=device(zz, yy, cc), device_id_type=MESH,
+        ).wait_recv()
+
+    def pieces(order):
+        return enumerate((WHOLE,) if order == 0 else PIECES)
+
+    def zq(order, i, piece, cc):
+        return q_copy((others[order], y, cc), i, piece, zq_send, zq_recv)
+
+    def yq(cc):
+        return q_copy((z, 1 - y, cc), 0, WHOLE, yq_send, yq_recv)
+
+    def pq():
+        return q_copy((z, y, 1 - core), 0, WHOLE, yq_send, pq_recv)
+
+    def forward(order, i, piece):
+        zz = others[order]
         return pltpu.make_async_remote_copy(
-            q_piece(c, cc), qbuf.at[c, y, z, core], yq_send.at[c, cc], yq_recv.at[c, core],
-            device_id=device(z, 1 - y, cc), device_id_type=MESH,
-        )
-
-    def yq_wait(c):
-        for cc in range(2):
-            pltpu.make_async_remote_copy(
-                q_piece(c, cc), qbuf.at[c, 1 - y, z, cc], yq_send.at[c, cc], yq_recv.at[c, cc],
-                device_id=device(z, 1 - y, cc), device_id_type=MESH,
-            ).wait_recv()
-
-    def pq(c):
-        return pltpu.make_async_remote_copy(
-            q_piece(c, 1 - core), qbuf.at[c, y, z, core], pq_send.at[c], pq_recv.at[c],
-            device_id=device(z, y, 1 - core), device_id_type=MESH,
-        )
-
-    def forward(c, zz):
-        return pltpu.make_async_remote_copy(
-            qbuf.at[c, y, zz], qbuf.at[c, y, zz], f_send.at[c, zz], f_recv.at[c, zz],
+            qbuf.at[y, zz, :, :, part(piece)], qbuf.at[y, zz, :, :, part(piece)],
+            f_send.at[i, zz], f_recv.at[i, zz],
             device_id=device(z, 1 - y, core), device_id_type=MESH,
         )
 
@@ -272,38 +277,59 @@
             device_id=device(z, y, 1 - core), device_id_type=MESH,
         )
 
-    for c in range(PIECES):
-        q_own(c).start()
+    q_own.start()
     for c in range(CHUNKS):
         for copy in reversed(kv_local(c)):
             copy.start()
     with jax.named_scope("enter"):
         q_in.wait()
-        pl.semaphore_wait(barrier, len(peers))
-
-    for c in range(PIECES):
-        for zz in reversed(others):
-            for cc in range(2):
-                zq(c, zz, cc).start()
-        for cc in range(2):
-            yq(c, cc).start()
-        pq(c).start()
-        if c == 0:
-            for copy in self_remote():
-                copy.start()
+        pl.semaphore_wait(barrier, len(peers) + 2 * middle)
+
+    @pl.when(middle == 1)
+    def spread():
+        pl.semaphore_signal(far.at[0], inc=1, device_id=device(near, y, core), device_id_type=MESH)
+        pl.semaphore_signal(far.at[1], inc=1, device_id=device(across, y, core), device_id_type=MESH)
+
+    for cc in range(2):
+        yq(cc).start()
+    for cc in range(2):
+        zq(0, 0, WHOLE, cc).start()
+    pq().start()
+    for copy in self_remote():
+        copy.start()
     for c in range(CHUNKS):
         for copy in reversed(kv_remote(c)):
             copy.start()
+    for order in (1, 2):
+        if order == 1:
+
+            @pl.when(middle == 0)
+            def await_second():
+                pl.semaphore_wait(far.at[0], 1)
+        else:
+            pl.semaphore_wait(far.at[1], 1)
+
+            @pl.when(middle == 1)
+            def pass_on():
+                pl.semaphore_signal(far.at[1], inc=1, device_id=device(near, y, core), device_id_type=MESH)
+
+        for i, piece in pieces(order):
+            for cc in range(2):
+                zq(order, i, piece, cc).start()
 
     for copy in small:
         copy.wait()
-    place = chip * docs + lax.broadcasted_iota(jnp.int32, (docs, LANE), 0)
-    bias_doc[...] = jnp.where(place < off_ref[0], 0.0, MASKED)
-    spot = lax.broadcasted_iota(jnp.int32, (selves, 2 * LANE), 1)
-    key_row = chip * selves + lax.broadcasted_iota(jnp.int32, (selves, 2 * LANE), 0)
+    place = lax.broadcasted_iota(jnp.int32, (docs, LANE), 0)
+    lane = lax.broadcasted_iota(jnp.int32, (docs, LANE), 1)
+    hidden = (chip * docs + place >= off_ref[0]) & (lane == 0)
+    key_mask[:docs, :] = jnp.where(hidden, MASKED, 0.0).astype(key_mask.dtype)
+    own = lane[:selves] == place[:selves] + 1
+    key_mask[docs:, :] = jnp.where(own, 1.0, 0.0).astype(key_mask.dtype)
+    spot, lane = place[: 2 * LANE], lane[: 2 * LANE]
     inner = spot % side
     row = ((inner // (2 * rows)) * 2 + jnp.where(spot < LANE, y, 1 - y)) * (2 * rows) + inner % (2 * rows)
-    bias_self[...] = jnp.where(key_row <= row, 0.0, MASKED)
+    later = (lane <= selves) & (chip * selves + lane - 1 > row)
+    row_mask[...] = jnp.where(lane == 0, 1.0, jnp.where(later, MASKED, 0.0)).astype(row_mask.dtype)
     ones = lax.broadcasted_iota(jnp.int32, (16, docs + LANE), 0) == 0
     ones = jnp.where(ones, 1.0, 0.0).astype(vt.dtype)
     for g in range(HALF_KVH):
@@ -327,65 +353,83 @@
             vt[c * GROUPS + g, :HD, docs:] = last.T.astype(vt.dtype)
 
     def relay(c):
-        for zz in others:
-            zq_wait(c, zz)
-            forward(c, zz).start()
+        for order in range(3):
+            for i, piece in pieces(order):
+                if i == c:
+                    for cc in range(2):
+                        q_wait((others[order], y, cc), i, piece, zq_send, zq_recv)
+                    forward(order, i, piece).start()
 
     factor = QSCALE ** (-0.5) * LOG2E
+    base = me // n
     tile = 256
-    per_piece = CHUNKS // PIECES
 
     def attend(c):
-        piece = c // per_piece
-        if c % per_piece == 0:
-            with jax.named_scope("queries"):
-                q_own(piece).wait()
-                pq(piece).wait_recv()
-                yq_wait(piece)
-                for zz in others:
-                    forward(piece, zz).wait_recv()
-        for g in range(GROUPS):
-            at = c * GROUPS + g
-            cols = slice(at * HD, (at + 1) * HD)
+        with jax.named_scope("queries"):
+            if c == 0:
+                q_own.wait()
+                q_wait((z, y, 1 - core), 0, WHOLE, yq_send, pq_recv)
+                for cc in range(2):
+                    q_wait((z, 1 - y, cc), 0, WHOLE, yq_send, yq_recv)
+            for order in range(3):
+                for i, piece in pieces(order):
+                    if piece[0] == c:
+                        forward(order, i, piece).wait_recv()
+
+        def load(g):
             pieces = []
             for yy in (y, 1 - y):
                 for j in range(PER_GROUP):
-                    h = ((c % per_piece) * GROUPS + g) * PER_GROUP + j
-                    block = qbuf[piece, yy, :, :, :, h * HD : (h + 1) * HD].astype(jnp.float32)
+                    h = (c * GROUPS + g) * PER_GROUP + j
+                    block = qbuf[yy, :, :, :, h * HD : (h + 1) * HD].astype(jnp.float32)
                     pieces.append(block.reshape(side, HD).astype(jnp.bfloat16))
-            query = jnp.concatenate(pieces, axis=0)
-            top = None
-            for start in list(range(0, docs, tile)) + [docs]:
-                size = tile if start < docs else selves
-                part = lax.dot_general(
-                    kbuf[start : start + size, cols], query, (((1,), (1,)), ((), ())),
-                    preferred_element_type=jnp.float32,
+            return jnp.concatenate([jnp.concatenate(pieces, axis=0), row_mask[...]], axis=1)
+
+        starts = list(range(0, docs, tile)) + [docs]
+        q_starts = list(range(0, docs, QK_TILE)) + [docs]
+
+        def score(g, query, start, top):
+            at = c * GROUPS + g
+            size = QK_TILE if start < docs else selves
+            span = slice(start, start + size)
+            key = jnp.concatenate([kbuf[span, at * HD : (at + 1) * HD], key_mask[span, :]], axis=1)
+            part = lax.dot_general(
+                key, query, (((1,), (1,)), ((), ())), preferred_element_type=jnp.float32
+            )
+            scores[base, at % 2, start : start + size, :] = part
+            most = jnp.max(part.reshape(size // 8, 8, 2 * LANE), axis=0)
+            return most if top is None else jnp.maximum(top, most)
+
+        def weigh(g, start, top, total):
+            at = c * GROUPS + g
+            size = span = tile if start < docs else selves
+            weights = jnp.exp2((scores[base, at % 2, start : start + size, :] - top) * factor)
+            if start == docs:
+                span = LANE
+                weights = jnp.concatenate(
+                    [weights, jnp.zeros((LANE - selves, 2 * LANE), jnp.float32)], axis=0
                 )
-                if start < docs:
-                    mask = bias_doc[start : start + size, :]
-                    part = part + jnp.concatenate([mask, mask], axis=1)
-                else:
-                    part = part + bias_self[...]
-                scores[at % 2, start : start + size, :] = part
-                most = jnp.max(part.reshape(size // 8, 8, 2 * LANE), axis=0)
-                top = most if top is None else jnp.maximum(top, most)
-            top = jnp.max(top, axis=0, keepdims=True)
-            total = None
-            for start in list(range(0, docs, tile)) + [docs]:
-                size = tile if start < docs else selves
-                part = scores[at % 2, start : start + size, :]
-                weights = jnp.exp2((part - top) * factor)
-                span = size
-                if start == docs:
-                    span = LANE
-                    weights = jnp.concatenate(
-                        [weights, jnp.zeros((LANE - selves, 2 * LANE), jnp.float32)], axis=0
-                    )
-                got = jnp.dot(
-                    vt[at, :, start : start + span], weights.astype(jnp.bfloat16),
-                    preferred_element_type=jnp.float32,
-                )
-                total = got if total is None else total + got
+            got = jnp.dot(
+                vt[at, :, start : start + span], weights.astype(jnp.bfloat16),
+                preferred_element_type=jnp.float32,
+            )
+            return got if total is None else total + got
+
+        def begin(g):
+            query, after = load(g), None
+            for start in q_starts:
+                after = score(g, query, start, after)
+            return after
+
+        after = begin(0)
+        for g in range(GROUPS):
+            top, total = jnp.max(after, axis=0, keepdims=True), None
+            if g + 1 < GROUPS and AHEAD:
+                after = begin(g + 1)
+            for start in starts:
+                total = weigh(g, start, top, total)
+            if g + 1 < GROUPS and not AHEAD:
+                after = begin(g + 1)
             top = top * factor
             den = total[HD : HD + 1]
             num = total[:HD]
@@ -474,14 +518,14 @@
         for c in range(CHUNKS):
             for copy in kv_remote(c):
                 copy.wait_send()
-        for c in range(PIECES):
-            pq(c).wait_send()
-            for cc in range(2):
-                yq(c, cc).wait_send()
-            for zz in others:
-                forward(c, zz).wait_send()
+        pq().wait_send()
+        for cc in range(2):
+            yq(cc).wait_send()
+        for order in range(3):
+            for i, piece in pieces(order):
+                forward(order, i, piece).wait_send()
                 for cc in range(2):
-                    zq(c, zz, cc).wait_send()
+                    zq(order, i, piece, cc).wait_send()
         for c in range(CHUNKS):
             p_copy(c).wait_send()
 
@@ -489,16 +533,17 @@
         with jax.named_scope(f"{name}#c={c}"):
             step(c)
 
+    run("turn", turn, 0)
     run("relay", relay, 0)
-    run("turn", turn, 0)
     run("turn", turn, 1)
+    run("turn", turn, 2)
     run("relay", relay, 1)
+    run("turn", turn, 3)
     for c in range(CHUNKS):
         run("attend", attend, c)
-        if c + 2 < CHUNKS:
-            run("turn", turn, c + 2)
-        if c > 0:
-            run("pair_up", pair_up, c - 1)
+        if c > 1:
+            run("pair_up", pair_up, c - 2)
+    run("pair_up", pair_up, CHUNKS - 2)
     run("pair_up", pair_up, CHUNKS - 1)
     with jax.named_scope("drain"):
         drain()
@@ -553,11 +598,11 @@
     docs, selves = 2 * doc, 2 * rows
     half_kv = HALF_KVH * HD
     wide = GROUPS * PER_GROUP * HD
-    q_wide = half_kv * PER_GROUP // PIECES
     vmem = pl.BlockSpec(memory_space=pltpu.VMEM)
     hbm = pl.BlockSpec(memory_space=pltpu.HBM)
     smem = pl.BlockSpec(memory_space=pltpu.SMEM)
     f32, bf16 = jnp.float32, jnp.bfloat16
+    pieces = len(PIECES)
     dma = pltpu.SemaphoreType.DMA
     return pl.pallas_call(
         functools.partial(fused_kernel, n),
@@ -566,14 +611,15 @@
         out_specs=vmem,
         scratch_shapes=[
             pltpu.VMEM((rows, H * HD), bf16),
-            pltpu.VMEM((PIECES, 2, length, 2, rows, q_wide), bf16),
+            pltpu.VMEM((2, length, 2, rows, half_kv * PER_GROUP), bf16),
             pltpu.VMEM((2, rows, half_kv), bf16),
             pltpu.VMEM((2, rows, half_kv), bf16),
             pltpu.VMEM((docs + selves, half_kv), bf16),
             pltpu.VMEM((HALF_KVH, HD + 16, docs + LANE), bf16),
-            pltpu.VMEM((docs, LANE), f32),
-            pltpu.VMEM((selves, 2 * LANE), f32),
-            pltpu.VMEM((2, docs + selves, 2 * LANE), f32),
+            pltpu.VMEM((docs + selves, LANE), bf16),
+            pltpu.VMEM((2 * LANE, LANE), bf16),
+            pltpu.VMEM((1, 2, docs + selves, 2 * LANE), f32),
+            pltpu.VMEM((1, docs + LANE, 2 * LANE), bf16),
             pltpu.VMEM((docs + selves, half_kv), bf16),
             pltpu.VMEM((CHUNKS, GROUPS * HD, LANE), f32),
             pltpu.VMEM((CHUNKS, STATS, LANE), f32),
@@ -582,19 +628,19 @@
             pltpu.VMEM((CHUNKS, length, 2 * rows, wide + LANE), WIRE),
             pltpu.VMEM((CHUNKS, length, 2 * rows, wide + LANE), WIRE),
             pltpu.VMEM((CHUNKS, rows, wide), bf16),
-            dma((PIECES + 1,)),
+            dma((2,)),
             dma((2,)),
             dma((2, CHUNKS)),
             dma((2, CHUNKS + 1)),
             dma((2, CHUNKS + 1)),
-            dma((PIECES, length, 2)),
-            dma((PIECES, length, 2)),
-            dma((PIECES, 2)),
-            dma((PIECES, 2)),
-            dma((PIECES,)),
-            dma((PIECES,)),
-            dma((PIECES, length)),
-            dma((PIECES, length)),
+            dma((pieces, length, 2)),
+            dma((pieces, length, 2)),
+            dma((1, length, 2)),
+            dma((1, length, 2)),
+            dma((1, length, 2)),
+            dma((pieces, length)),
+            dma((pieces, length)),
+            pltpu.SemaphoreType.REGULAR((2,)),
             dma((CHUNKS,)),
             dma((CHUNKS,)),
             dma((CHUNKS, length)),

time: 34.4 us -> 31.6 us (0.919)
  Pallas kernels: 32.3 us -> 29.5 us
    pallas_call x1, Pallas kernels: 32.3 us -> 29.5 us  [fused(): pl.pallas_call(functools.partial(fused_kernel, n), out_shape=jax.ShapeDty...]
where the time goes in v3:
time: 31.6 us; the launch traced here: 31.4 us
  Pallas kernels  29.5 us (93%)
  between operations  1.3 us (4%)
  local copies, waits for them, and re-layouts  0.63 us (2%)
    pallas_call x1, Pallas kernels, fused(): pl.pallas_call(functools.partial(fused_kernel, n), out_shape=jax.ShapeDty...  29.5 us
    unnamed x1, local copies, waits for them, and re-layouts  0.63 us

profile of v3, /device:TPU:0, one launch (start us, length us, event | category | flops | bytes accessed | tf_op | source)
XLA Modules:
  0.0 31.4 jit_solution(3580325751570628017)
XLA Ops:
  1.3 29.5 %shard_map.73 = bf16[8,4096]{1,0:T(8,128)(2,1)S(1)} custom-call(bf16[8,4096]{1,0:T(8,128)(2,1)} %q_hbm.1, bf16[8,2048]{1,0:T(8,128)(2,1)} %qk_hbm.1, bf16[8,2048]{1,0:T(8,128)(2,1)} %qv_hbm.1, bf16[512,2048]{1,0:T(8,128)(2,1)} %k_hbm.1, bf16[512,2048]{1,0:T(8,128)(2,1)} %v_hbm.1, s32[1]{0:T(128)S(6)} %copy.9.len_ref, s32[1]{0:T(128)S(6)} %copy.10.off_ref), custom_call_target="tpu_custom_call" | custom-call | tf_op jit(solution)/shard_map/pallas_call | solution.py:607
  30.8 0.6 %copy.11 = bf16[8,4096]{1,0:T(8,128)(2,1)} copy(bf16[8,4096]{1,0:T(8,128)(2,1)S(1)} %shard_map.73) | data formatting | bytes 131072

commit v4 on v3

v4 whole, which is shorter than its diff:
```python
import functools
import math

import jax
import jax.numpy as jnp
from jax import lax
from jax.experimental import pallas as pl
from jax.experimental.pallas import tpu as pltpu
from jax.sharding import PartitionSpec as P

H = 32
KVH = 16
HD = 128
QSCALE = 144
QL = 128
NQ = 1


MASKED = -1e30


def row_tables(start, count, lengths, offsets):
    rows = start + jnp.arange(count, dtype=jnp.int32)
    question = rows // QL
    position = rows % QL
    owner_table = question[:, None] == jnp.arange(NQ, dtype=jnp.int32)[None, :]
    row_length = jnp.sum(jnp.where(owner_table, lengths[None, :], 0), axis=1)
    row_offset = jnp.sum(jnp.where(owner_table, offsets[None, :], 0), axis=1)
    return (question, position, position < row_length, row_offset)


def local(queries, question_keys, question_values, doc_keys, doc_values, lengths, offsets):
    rows_local = queries.shape[0]
    doc_local = doc_keys.shape[0]
    device_count = lax.axis_size("seq")
    device_index = lax.axis_index("seq")
    total_rows = rows_local * device_count
    per_group = H // KVH
    factor_q = QSCALE ** (-0.5)
    key_doc = doc_keys.reshape(doc_local, KVH, HD)
    value_doc = doc_values.reshape(doc_local, KVH, HD)
    key_self = question_keys.reshape(rows_local, KVH, HD)
    value_self = question_values.reshape(rows_local, KVH, HD)
    doc_places = device_index * doc_local + jnp.arange(doc_local, dtype=jnp.int32)
    self_rows = device_index * rows_local + jnp.arange(rows_local, dtype=jnp.int32)
    whole = lax.all_gather(queries, "seq", axis=0, tiled=True)
    block_rows = math.gcd(total_rows, 512)
    block_count = total_rows // block_rows

    def one_block(start):
        piece = whole.reshape(block_rows, KVH, per_group, HD)
        question, position, live_rows, row_offset = row_tables(start, block_rows, lengths, offsets)
        mask_doc = live_rows[:, None] & (doc_places[None, :] < row_offset[:, None])
        mask_self = (
            live_rows[:, None]
            & (self_rows[None, :] // QL == question[:, None])
            & (self_rows[None, :] % QL <= position[:, None])
        )
        mask_doc = mask_doc[:, None, None, :]
        mask_self = mask_self[:, None, None, :]
        scores_doc = (
            jnp.einsum("rgjd,kgd->rgjk", piece, key_doc, preferred_element_type=jnp.float32)
            * factor_q
        )
        scores_self = (
            jnp.einsum("rgjd,kgd->rgjk", piece, key_self, preferred_element_type=jnp.float32)
            * factor_q
        )
        scores_doc = jnp.where(mask_doc, scores_doc, MASKED)
        scores_self = jnp.where(mask_self, scores_self, MASKED)
        block_top = jnp.maximum(jnp.max(scores_doc, axis=-1), jnp.max(scores_self, axis=-1))
        weights_doc = jnp.where(mask_doc, jnp.exp(scores_doc - block_top[..., None]), 0.0).astype(
            jnp.bfloat16
        )
        weights_self = jnp.where(
            mask_self, jnp.exp(scores_self - block_top[..., None]), 0.0
        ).astype(jnp.bfloat16)
        block_den = jnp.sum(weights_doc.astype(jnp.float32), axis=-1) + jnp.sum(
            weights_self.astype(jnp.float32), axis=-1
        )
        block_num = jnp.einsum(
            "rgjk,kgd->rgjd", weights_doc, value_doc, preferred_element_type=jnp.float32
        )
        block_num = block_num + jnp.einsum(
            "rgjk,kgd->rgjd", weights_self, value_self, preferred_element_type=jnp.float32
        )
        return (
            block_num.reshape(block_rows, H * HD),
            block_top.reshape(block_rows, H),
            block_den.reshape(block_rows, H),
        )

    starts = jnp.arange(block_count, dtype=jnp.int32) * block_rows
    numer, row_top, denom = lax.map(one_block, starts)
    numer = numer.reshape(total_rows, H * HD)
    row_top = row_top.reshape(total_rows, H)
    denom = denom.reshape(total_rows, H)
    got_num, got_top, got_den = (
        lax.all_to_all(numer[None], "seq", split_axis=1, concat_axis=0, tiled=True),
        lax.all_to_all(row_top[None], "seq", split_axis=1, concat_axis=0, tiled=True),
        lax.all_to_all(denom[None], "seq", split_axis=1, concat_axis=0, tiled=True),
    )
    overall = jnp.max(got_top, axis=0)
    rescale = jnp.exp(got_top - overall[None])
    total_num = jnp.sum(
        got_num.reshape(device_count, rows_local, H, HD) * rescale[:, :, :, None], axis=0
    )
    total_den = jnp.sum(got_den * rescale, axis=0)
    question, position, live_rows, row_offset = row_tables(
        device_index * rows_local, rows_local, lengths, offsets
    )
    safe_den = jnp.where(live_rows[:, None], total_den, 1.0)
    result = (total_num / safe_den[:, :, None]).reshape(rows_local, H * HD)
    return jnp.where(live_rows[:, None], result, 0.0).astype(jnp.bfloat16)


MESH = pl.DeviceIdType.MESH
LANE = 128
CHUNKS = ((0, 2), (2, 2), (4, 2), (6, 2))
GROUPS = 2
PIECES = ((0, 2), (2, 8))
WHOLE = (0, 8)
LOG2E = math.log2(math.e)
WIRE = jnp.int16
WIRE_TOP = 32767.0
HALF_KVH = KVH // 2
PER_GROUP = H // KVH
STATS = 8
QK_TILE = 256


def fused_kernel(
    n, q_hbm, qk_hbm, qv_hbm, k_hbm, v_hbm, len_ref, off_ref, o_ref,
    qown, qbuf, selfs, kv, vt, key_mask, row_mask, scores,
    nkeep, skeep, nsend, narr, wsend, warr, osend, okeep,
    local_sem, kv_sem, kv_recv, once_send, once_recv, zq_recv, f_recv, r_recv, far, p_recv, w_recv,
):
    length = n // 4
    rows = q_hbm.shape[0]
    doc = k_hbm.shape[0]
    docs = 2 * doc
    selves = 2 * rows
    half_kv = HALF_KVH * HD
    half_q = half_kv * PER_GROUP
    unit = PER_GROUP * HD
    side = length * 2 * rows
    me = lax.axis_index("seq")
    core = lax.rem(me, 2)
    chip = me // 2
    y = lax.rem(chip, 2)
    z = chip // 2
    others = (z + 1 - 2 * lax.rem(z, 2), 2 - z // 2, 3 - 3 * (z // 2))

    def device(zz, yy, cc):
        return {"seq": (zz * 2 + yy) * 2 + cc}

    middle = (lax.rem(z, length - 1) + 1) // 2
    across = 1 + lax.rem(z, 2)
    near = others[0]
    kv_sent, self_sent, q_sent, pq_sent, f_sent, r_sent, p_sent, w_sent, o_sent = range(9)
    self_got, yq_got, pq_got, o_got = range(4)

    def await_bytes(ref, sem):
        pltpu.make_async_copy(ref, ref, sem).wait()

    barrier = pltpu.get_barrier_semaphore()
    peers = [device(z, y, 1 - core)] + [device(z, 1 - y, cc) for cc in range(2)]
    peers += [device(near, y, cc) for cc in range(2)]
    for peer in peers:
        pl.semaphore_signal(barrier, inc=1, device_id=peer, device_id_type=MESH)

    @pl.when(middle == 1)
    def greet():
        for cc in range(2):
            pl.semaphore_signal(barrier, inc=1, device_id=device(across, y, cc), device_id_type=MESH)

    q_in = pltpu.make_async_copy(q_hbm, qown, local_sem.at[0])
    q_in.start()
    for i, a in enumerate((qk_hbm, qv_hbm)):
        pltpu.make_async_copy(
            a.at[:, pl.ds(core * half_kv, half_kv)], selfs.at[i, core], local_sem.at[2]
        ).start()

    def part(piece):
        return pl.ds(piece[0] * unit, (piece[1] - piece[0]) * unit)

    def o_local(c):
        cols = pl.ds(CHUNKS[c][0] * unit, CHUNKS[c][1] * unit)
        to = pl.ds(core * half_q + CHUNKS[c][0] * unit, CHUNKS[c][1] * unit)
        return pltpu.make_async_copy(okeep.at[:, cols], o_ref.at[:, to], local_sem.at[3])

    q_own = pltpu.make_async_copy(q_hbm.at[:, pl.ds(core * half_q, half_q)], qbuf.at[y, z, core], local_sem.at[1])

    def kv_cols(side_core, c):
        return pl.ds(side_core * half_kv + CHUNKS[c][0] * HD, CHUNKS[c][1] * HD)

    def kv_part(side_core, c):
        return kv.at[:, pl.ds(side_core * doc, doc), kv_cols(0, c)]

    def kv_local(c):
        at = pl.ds(core * doc, doc)
        return [
            pltpu.make_async_copy(a.at[:, kv_cols(core, c)], kv.at[i, at, kv_cols(0, c)], kv_sem.at[c])
            for i, a in enumerate((k_hbm, v_hbm))
        ]

    def kv_remote(c):
        at = pl.ds(core * doc, doc)
        return [
            pltpu.make_async_remote_copy(
                a.at[:, kv_cols(1 - core, c)], kv.at[i, at, kv_cols(0, c)],
                once_send.at[kv_sent], kv_recv.at[c],
                device_id=device(z, y, 1 - core), device_id_type=MESH,
            )
            for i, a in enumerate((k_hbm, v_hbm))
        ]

    def self_remote():
        cols = pl.ds((1 - core) * half_kv, half_kv)
        return [
            pltpu.make_async_remote_copy(
                a.at[:, cols], selfs.at[i, core], once_send.at[self_sent], once_recv.at[self_got],
                device_id=device(z, y, 1 - core), device_id_type=MESH,
            )
            for i, a in enumerate((qk_hbm, qv_hbm))
        ]

    def q_copy(where, piece, send_sem, recv_sem):
        zz, yy, cc = where
        return pltpu.make_async_remote_copy(
            qown.at[:, pl.ds(cc * half_q + piece[0] * unit, (piece[1] - piece[0]) * unit)],
            qbuf.at[y, z, core, :, part(piece)], send_sem, recv_sem,
            device_id=device(zz, yy, cc), device_id_type=MESH,
        )

    def zq(order, i, piece, cc):
        to = 0 if order == 0 else 2 - middle
        return q_copy((others[order], y, cc), piece, once_send.at[q_sent], zq_recv.at[i, to])

    def yq(cc):
        return q_copy((z, 1 - y, cc), WHOLE, once_send.at[q_sent], once_recv.at[yq_got])

    def pq():
        return q_copy((z, y, 1 - core), WHOLE, once_send.at[pq_sent], once_recv.at[pq_got])

    def forward(order, i, piece):
        zz = others[order]
        return pltpu.make_async_remote_copy(
            qbuf.at[y, zz, :, :, part(piece)], qbuf.at[y, zz, :, :, part(piece)],
            once_send.at[f_sent], f_recv.at[i, order],
            device_id=device(z, 1 - y, core), device_id_type=MESH,
        )

    def along(order, i, piece):
        zz = others[order]
        return pltpu.make_async_remote_copy(
            qbuf.at[y, zz, :, :, part(piece)], qbuf.at[y, zz, :, :, part(piece)],
            once_send.at[r_sent], r_recv.at[i, order - 1],
            device_id=device(near, y, core), device_id_type=MESH,
        )

    def p_copy(c):
        return pltpu.make_async_remote_copy(
            nsend.at[c, pl.ds(0, CHUNKS[c][1] * HD + 16)], narr.at[c, pl.ds(0, CHUNKS[c][1] * HD + 16)],
            once_send.at[p_sent], p_recv.at[c],
            device_id=device(z, 1 - y, core), device_id_type=MESH,
        )

    def w_copy(c, zz):
        return pltpu.make_async_remote_copy(
            wsend.at[c, zz, :, pl.ds(0, CHUNKS[c][1] * unit + LANE)],
            warr.at[c, z, :, pl.ds(0, CHUNKS[c][1] * unit + LANE)], once_send.at[w_sent], w_recv.at[c],
            device_id=device(zz, y, core), device_id_type=MESH,
        )

    def o_copy(c):
        return pltpu.make_async_remote_copy(
            osend.at[:, pl.ds(CHUNKS[c][0] * unit, CHUNKS[c][1] * unit)],
            o_ref.at[:, pl.ds(core * half_q + CHUNKS[c][0] * unit, CHUNKS[c][1] * unit)],
            once_send.at[o_sent], once_recv.at[o_got],
            device_id=device(z, y, 1 - core), device_id_type=MESH,
        )

    q_own.start()
    for c in range(len(CHUNKS)):
        for copy in reversed(kv_local(c)):
            copy.start()
    with jax.named_scope("enter"):
        q_in.wait()
        pl.semaphore_wait(barrier, len(peers) + 2 * middle)

    @pl.when(middle == 1)
    def spread():
        for cc in range(2):
            pl.semaphore_signal(far, inc=1, device_id=device(near, y, cc), device_id_type=MESH)

    for cc in range(2):
        yq(cc).start()
    def send(order, i):
        for cc in range(2):
            zq(order, i, PIECES[i], cc).start()

    early = z < length // 2
    rest = range(1, len(PIECES))
    send(0, 0)

    @pl.when(early)
    def near_rest():
        for i in rest:
            send(0, i)

    pq().start()
    for copy in self_remote():
        copy.start()
    for c in range(len(CHUNKS)):
        for copy in reversed(kv_remote(c)):
            copy.start()

    @pl.when(middle == 0)
    def await_second():
        pl.semaphore_wait(far, 2)

    send(1, 0)

    @pl.when(z >= length // 2)
    def late_rest():
        for i in rest:
            send(0, i)

    for i in rest:
        send(1, i)

    await_bytes(selfs.at[0], local_sem.at[2])
    place = lax.broadcasted_iota(jnp.int32, (docs, LANE), 0)
    lane = lax.broadcasted_iota(jnp.int32, (docs, LANE), 1)
    hidden = (chip * docs + place >= off_ref[0]) & (lane == 0)
    key_mask[:docs, :] = jnp.where(hidden, MASKED, 0.0).astype(key_mask.dtype)
    own = lane[:selves] == place[:selves] + 1
    key_mask[docs:, :] = jnp.where(own, 1.0, 0.0).astype(key_mask.dtype)
    spot, lane = place[: 2 * LANE], lane[: 2 * LANE]
    inner = spot % side
    row = ((inner // (2 * rows)) * 2 + jnp.where(spot < LANE, y, 1 - y)) * (2 * rows) + inner % (2 * rows)
    later = (lane <= selves) & (chip * selves + lane - 1 > row)
    row_mask[...] = jnp.where(lane == 0, 1.0, jnp.where(later, MASKED, 0.0)).astype(row_mask.dtype)
    ones = lax.broadcasted_iota(jnp.int32, (16, docs + LANE), 0) == 0
    ones = jnp.where(ones, 1.0, 0.0).astype(vt.dtype)
    for g in range(HALF_KVH):
        vt[g, HD:, :] = ones
    await_bytes(selfs.at[0], once_recv.at[self_got])
    for i in range(2):
        kv[i, docs:, :] = selfs[i].astype(jnp.float32).reshape(selves, half_kv).astype(kv.dtype)

    def turn(c):
        with jax.named_scope("kv"):
            await_bytes(kv_part(core, c), kv_sem.at[c])
            await_bytes(kv_part(1 - core, c), kv_recv.at[c])
        for g in range(CHUNKS[c][0], sum(CHUNKS[c])):
            cols = slice(g * HD, (g + 1) * HD)
            vt[g, :HD, :docs] = kv[1, :docs, cols].T
            last = kv[1, docs:, cols].astype(jnp.float32)
            last = jnp.concatenate([last, jnp.zeros((LANE - selves, HD), jnp.float32)], axis=0)
            vt[g, :HD, docs:] = last.T.astype(vt.dtype)

    def take(order, i):
        zz = others[order]

        block = qbuf.at[y, zz, :, :, part(PIECES[i])]
        if order == 0:
            await_bytes(block, zq_recv.at[i, 0])
        else:

            @pl.when(middle == 1)
            def hand_on():
                await_bytes(block, zq_recv.at[i, order])
                along(order, i, PIECES[i]).start()

            @pl.when(middle == 0)
            def handed():
                await_bytes(block, r_recv.at[i, order - 1])

        forward(order, i, PIECES[i]).start()

    def relay(c):
        take(0, c)
        if c == 0:

            @pl.when(early)
            def near_too():
                take(0, 1)

        else:
            return
        take(1, 0)
        take(2, 0)

    def relay_rest():
        @pl.when(z >= length // 2)
        def near_now():
            take(0, 1)

        take(1, 1)
        take(2, 1)

    factor = QSCALE ** (-0.5) * LOG2E
    base = me // n
    tile = 256

    def attend(c):
        first, count = CHUNKS[c]
        with jax.named_scope("queries"):
            if c == 0:
                q_own.wait()
                await_bytes(qbuf.at[y, z, 1 - core], once_recv.at[pq_got])
                await_bytes(qbuf.at[1 - y, z], once_recv.at[yq_got])
            for i, piece in enumerate(PIECES):
                if piece[0] == CHUNKS[c][0]:
                    for order in range(3):
                        await_bytes(
                            qbuf.at[1 - y, others[order], :, :, part(piece)], f_recv.at[i, order]
                        )

        def load(g):
            pieces = []
            for yy in (y, 1 - y):
                for j in range(PER_GROUP):
                    h = (first + g) * PER_GROUP + j
                    block = qbuf[yy, :, :, :, h * HD : (h + 1) * HD].astype(jnp.float32)
                    pieces.append(block.reshape(side, HD).astype(jnp.bfloat16))
            return jnp.concatenate([jnp.concatenate(pieces, axis=0), row_mask[...]], axis=1)

        starts = list(range(0, docs, tile)) + [docs]
        q_starts = list(range(0, docs, QK_TILE)) + [docs]

        def score(g, query, start, top):
            at = first + g
            size = QK_TILE if start < docs else selves
            span = slice(start, start + size)
            key = jnp.concatenate([kv[0, span, at * HD : (at + 1) * HD], key_mask[span, :]], axis=1)
            part = lax.dot_general(
                key, query, (((1,), (1,)), ((), ())), preferred_element_type=jnp.float32
            )
            scores[base, at % 2, start : start + size, :] = part
            most = jnp.max(part.reshape(size // 8, 8, 2 * LANE), axis=0)
            return most if top is None else jnp.maximum(top, most)

        def weigh(g, start, top, total):
            at = first + g
            size = span = tile if start < docs else selves
            weights = jnp.exp2((scores[base, at % 2, start : start + size, :] - top) * factor)
            if start == docs:
                span = LANE
                weights = jnp.concatenate(
                    [weights, jnp.zeros((LANE - selves, 2 * LANE), jnp.float32)], axis=0
                )
            got = jnp.dot(
                vt[at, :, start : start + span], weights.astype(jnp.bfloat16),
                preferred_element_type=jnp.float32,
            )
            return got if total is None else total + got

        def begin(g):
            query, after = load(g), None
            for start in q_starts:
                after = score(g, query, start, after)
            return after

        after = begin(0)
        for g in range(count):
            top, total = jnp.max(after, axis=0, keepdims=True), None
            if g + 1 < count:
                after = begin(g + 1)
            for start in starts:
                total = weigh(g, start, top, total)
            top = top * factor
            den = total[HD : HD + 1]
            num = total[:HD]
            nkeep[c, g * HD : (g + 1) * HD, :] = num[:, :LANE]
            skeep[c, 2 * g : 2 * g + 1, :] = top[:, :LANE]
            skeep[c, 2 * g + 1 : 2 * g + 2, :] = den[:, :LANE]
            out = num[:, LANE:]
            largest = jnp.maximum(jnp.max(jnp.abs(out), axis=0, keepdims=True), 1e-30)
            nsend[c, g * HD : (g + 1) * HD, :] = encode(out * (WIRE_TOP / largest))
            skeep[c, 4 + g : 5 + g, :] = top[:, LANE:] + log2(den[:, LANE:])
            skeep[c, 6 + g : 7 + g, :] = top[:, LANE:] + log2(largest)
        logs = split(skeep[c, 4:8, :])
        logs = jnp.concatenate([logs, jnp.zeros((8, LANE), jnp.float32)], axis=0)
        nsend[c, count * HD : count * HD + 16, :] = encode(logs)
        p_copy(c).start()

    def pair_up(c):
        count = CHUNKS[c][1]
        wide = count * unit
        with jax.named_scope("pair"):
            await_bytes(narr.at[c], p_recv.at[c])
        logs = decode(narr[c, count * HD : count * HD + 16, :])
        logs = logs[:4] * COARSE + logs[4:8] * FINE
        mass, span = [], []
        for g in range(count):
            top_a, den_a = skeep[c, 2 * g : 2 * g + 1, :], skeep[c, 2 * g + 1 : 2 * g + 2, :]
            mass_b, span_b = logs[g : g + 1], logs[2 + g : 3 + g]
            top = jnp.maximum(top_a, mass_b)
            fa = jnp.exp2(top_a - top)
            den = den_a * fa + jnp.exp2(mass_b - top)
            fb = jnp.exp2(span_b - top) * (1.0 / WIRE_TOP)
            at = slice(g * HD, (g + 1) * HD)
            num = nkeep[c, at, :] * fa + decode(narr[c, at, :]) * fb
            largest = jnp.maximum(jnp.max(jnp.abs(num), axis=0, keepdims=True), 1e-30)
            codes = encode((num * (WIRE_TOP / largest)).T)
            for j in range(PER_GROUP):
                h = g * PER_GROUP + j
                wsend[c, :, :, h * HD : (h + 1) * HD] = codes[j * side : (j + 1) * side].reshape(
                    length, 2 * rows, HD
                )
            mass.append(top + log2(den))
            span.append(top + log2(largest))
        spare = [jnp.zeros((1, LANE), jnp.float32)] * (GROUPS - count)
        table = split(jnp.concatenate(mass + spare + span + spare, axis=0))
        table = jnp.concatenate([table, jnp.zeros((LANE - 8, LANE), jnp.float32)], axis=0)
        table = encode(table.T)
        for j in range(PER_GROUP):
            wsend[c, :, :, wide + 8 * j : wide + 8 * j + 8] = table[j * side : (j + 1) * side, :8].reshape(
                length, 2 * rows, 8
            )
        for zz in reversed(others):
            w_copy(c, zz).start()
        warr[c, z] = wsend[c, z]

    def finish(c):
        first, count = CHUNKS[c]
        wide = count * unit
        with jax.named_scope("parts"):
            await_bytes(warr.at[c, pl.ds(0, length - 1)], w_recv.at[c])
        logs = []
        for k in range(length):
            block = decode(warr[c, k, :, wide : wide + LANE])
            logs.append(block * COARSE + pltpu.roll(block, LANE - 4, 1) * FINE)
        most = functools.reduce(jnp.maximum, logs)
        den = sum(jnp.exp2(x - most) for x in logs)
        most, den = pltpu.roll(most, 2, 1), pltpu.roll(den, 2, 1)
        share = 1.0 / (den * WIRE_TOP)
        coefs = [jnp.exp2(x - most) * share for x in logs]
        mine = chip * selves + lax.broadcasted_iota(jnp.int32, (selves, HD), 0)
        live = mine < len_ref[0]
        for g in range(count):
            for j in range(PER_GROUP):
                h = g * PER_GROUP + j
                at = 8 * j + 2 + g
                acc = None
                for k in range(length):
                    term = decode(warr[c, k, :, h * HD : (h + 1) * HD]) * coefs[k][:, at : at + 1]
                    acc = term if acc is None else acc + term
                acc = jnp.where(live, acc, 0.0)
                kept = jnp.where(core == 0, acc[:rows], acc[rows:])
                sent = jnp.where(core == 0, acc[rows:], acc[:rows])
                to = first * unit + h * HD
                okeep[:, to : to + HD] = kept.astype(o_ref.dtype)
                osend[:, first * unit + h * HD : first * unit + (h + 1) * HD] = sent.astype(o_ref.dtype)
        o_copy(c).start()
        o_local(c).start()

    def drain():
        await_bytes(kv.at[:, pl.ds(0, doc), :], once_send.at[kv_sent])
        await_bytes(selfs.at[0], once_send.at[self_sent])
        await_bytes(qown.at[:, pl.ds(0, half_q)], once_send.at[pq_sent])
        await_bytes(qbuf.at[0, pl.ds(0, 3)], once_send.at[q_sent])
        await_bytes(qbuf.at[0, pl.ds(0, 3)], once_send.at[f_sent])

        @pl.when(middle == 1)
        def handed_on():
            await_bytes(qbuf.at[0, pl.ds(0, 2)], once_send.at[r_sent])

        await_bytes(nsend, once_send.at[p_sent])

    def run(name, step, c):
        with jax.named_scope(f"{name}#c={c}"):
            step(c)

    run("turn", turn, 0)
    run("relay", relay, 0)
    for c in range(1, len(CHUNKS) - 1):
        run("turn", turn, c)
    with jax.named_scope("relay_rest"):
        relay_rest()
    run("turn", turn, len(CHUNKS) - 1)
    for c in range(len(CHUNKS)):
        run("attend", attend, c)
        if c > 1:
            run("pair_up", pair_up, c - 2)
    for c in range(len(CHUNKS) - 2, len(CHUNKS)):
        run("pair_up", pair_up, c)
    with jax.named_scope("drain"):
        drain()
    for c in range(len(CHUNKS)):
        run("finish", finish, c)
    with jax.named_scope("last"):
        await_bytes(wsend.at[:, pl.ds(0, length - 1)], once_send.at[w_sent])
        await_bytes(osend, once_send.at[o_sent])
        await_bytes(okeep, local_sem.at[3])
        await_bytes(osend, once_recv.at[o_got])


COARSE = 2.0 ** -5
FINE = 2.0 ** -20


def split(x):
    x = jnp.maximum(x, -1000.0)
    high = jnp.round(x * (1.0 / COARSE))
    return jnp.concatenate([high, (x - high * COARSE) * (1.0 / FINE)], axis=0)


def log2(x):
    return jnp.log(x) * LOG2E


def encode(x):
    return jnp.round(x).astype(jnp.int32).astype(WIRE)


def decode(x):
    return x.astype(jnp.int32).astype(jnp.float32)


def fused(n, queries, question_keys, question_values, doc_keys, doc_values, lengths, offsets):
    rows = queries.shape[0]
    doc = doc_keys.shape[0]
    if (
        NQ != 1 or n != 16 or rows % 8 or n * rows * PER_GROUP != 2 * LANE
        or doc % LANE or doc > 1024 or n * rows != QL
    ):
        return local(
            queries, question_keys, question_values, doc_keys, doc_values, lengths, offsets
        )
    operands = (queries, question_keys, question_values, doc_keys, doc_values)
    length = n // 4
    docs, selves = 2 * doc, 2 * rows
    half_kv = HALF_KVH * HD
    wide = GROUPS * PER_GROUP * HD
    hbm = pl.BlockSpec(memory_space=pltpu.HBM)
    smem = pl.BlockSpec(memory_space=pltpu.SMEM)
    f32, bf16 = jnp.float32, jnp.bfloat16
    pieces, chunks = len(PIECES), len(CHUNKS)
    dma = pltpu.SemaphoreType.DMA
    return pl.pallas_call(
        functools.partial(fused_kernel, n),
        out_shape=jax.ShapeDtypeStruct(queries.shape, bf16),
        in_specs=[hbm] * 5 + [smem] * 2,
        out_specs=pl.BlockSpec(memory_space=pl.ANY),
        scratch_shapes=[
            pltpu.VMEM((rows, H * HD), bf16),
            pltpu.VMEM((2, length, 2, rows, half_kv * PER_GROUP), bf16),
            pltpu.VMEM((2, 2, rows, half_kv), bf16),
            pltpu.VMEM((2, docs + selves, half_kv), bf16),
            pltpu.VMEM((HALF_KVH, HD + 16, docs + LANE), bf16),
            pltpu.VMEM((docs + selves, LANE), bf16),
            pltpu.VMEM((2 * LANE, LANE), bf16),
            pltpu.VMEM((1, 2, docs + selves, 2 * LANE), f32),
            pltpu.VMEM((chunks, GROUPS * HD, LANE), f32),
            pltpu.VMEM((chunks, STATS, LANE), f32),
            pltpu.VMEM((chunks, GROUPS * HD + 16, LANE), WIRE),
            pltpu.VMEM((chunks, GROUPS * HD + 16, LANE), WIRE),
            pltpu.VMEM((chunks, length, 2 * rows, wide + LANE), WIRE),
            pltpu.VMEM((chunks, length, 2 * rows, wide + LANE), WIRE),
            pltpu.VMEM((rows, half_kv * PER_GROUP), bf16),
            pltpu.VMEM((rows, half_kv * PER_GROUP), bf16),
            dma((4,)),
            dma((chunks,)),
            dma((chunks,)),
            dma((9,)),
            dma((4,)),
            dma((pieces, 3)),
            dma((pieces, 3)),
            dma((pieces, 2)),
            pltpu.SemaphoreType.REGULAR,
            dma((chunks,)),
            dma((chunks,)),
        ],
        compiler_params=pltpu.CompilerParams(
            collective_id=0, has_side_effects=True, vmem_limit_bytes=24 * 1024 * 1024
        ),
    )(*(pltpu.with_memory_space_constraint(x, pltpu.HBM) for x in operands), lengths, offsets)


def solution(mesh):
    placed = (
        P(("grp", "seq"), None),
        P(("grp", "seq"), None),
        P(("grp", "seq"), None),
        P(("grp", "seq"), None),
        P(("grp", "seq"), None),
        P("grp"),
        P("grp"),
    )
    return jax.shard_map(
        functools.partial(fused, mesh.shape["seq"]),
        mesh=mesh, in_specs=placed, out_specs=P(("grp", "seq"), None), check_vma=False,
    )
```

time: 31.6 us -> 30.7 us (0.972)
  Pallas kernels: 29.5 us -> 28.6 us
    pallas_call x1, Pallas kernels: 29.5 us -> 28.6 us  [fused(): pl.pallas_call(functools.partial(fused_kernel, n), out_shape=jax.ShapeDty...]
where the time goes in v4:
time: 30.7 us; the launch traced here: 30.5 us
  Pallas kernels  28.6 us (93%)
  between operations  1.3 us (4%)
  local copies, waits for them, and re-layouts  0.63 us (2%)
    pallas_call x1, Pallas kernels, fused(): pl.pallas_call(functools.partial(fused_kernel, n), out_shape=jax.ShapeDty...  28.6 us
    unnamed x1, local copies, waits for them, and re-layouts  0.63 us

profile of v4, /device:TPU:0, one launch (start us, length us, event | category | flops | bytes accessed | tf_op | source)
XLA Modules:
  0.0 30.5 jit_solution(9517093209098156185)
XLA Ops:
  1.3 28.6 %shard_map.73 = bf16[8,4096]{1,0:T(8,128)(2,1)S(1)} custom-call(bf16[8,4096]{1,0:T(8,128)(2,1)} %q_hbm.1, bf16[8,2048]{1,0:T(8,128)(2,1)} %qk_hbm.1, bf16[8,2048]{1,0:T(8,128)(2,1)} %qv_hbm.1, bf16[512,2048]{1,0:T(8,128)(2,1)} %k_hbm.1, bf16[512,2048]{1,0:T(8,128)(2,1)} %v_hbm.1, s32[1]{0:T(128)S(6)} %copy.9.len_ref, s32[1]{0:T(128)S(6)} %copy.10.off_ref), custom_call_target="tpu_custom_call" | custom-call | tf_op jit(solution)/shard_map/pallas_call | solution.py:644
  29.9 0.6 %copy.11 = bf16[8,4096]{1,0:T(8,128)(2,1)} copy(bf16[8,4096]{1,0:T(8,128)(2,1)S(1)} %shard_map.73) | data formatting | bytes 131072

commit v5 on v4

--- a/solution.py
+++ b/solution.py
@@ -118,7 +118,7 @@
 LANE = 128
 CHUNKS = ((0, 2), (2, 2), (4, 2), (6, 2))
 GROUPS = 2
-PIECES = ((0, 2), (2, 8))
+PIECES = ((0, 2), (2, 4), (4, 8))
 WHOLE = (0, 8)
 LOG2E = math.log2(math.e)
 WIRE = jnp.int16
@@ -322,13 +322,13 @@
 
     send(1, 0)
 
+    for i in rest:
+        send(1, i)
+
     @pl.when(z >= length // 2)
     def late_rest():
         for i in rest:
             send(0, i)
-
-    for i in rest:
-        send(1, i)
 
     await_bytes(selfs.at[0], local_sem.at[2])
     place = lax.broadcasted_iota(jnp.int32, (docs, LANE), 0)
@@ -380,26 +380,33 @@
 
         forward(order, i, PIECES[i]).start()
 
-    def relay(c):
-        take(0, c)
-        if c == 0:
-
-            @pl.when(early)
-            def near_too():
-                take(0, 1)
-
-        else:
-            return
+    def relay():
+        take(0, 0)
+
+        @pl.when(early)
+        def near_too():
+            for i in rest:
+                take(0, i)
+
         take(1, 0)
         take(2, 0)
 
     def relay_rest():
-        @pl.when(z >= length // 2)
+        late = z >= length // 2
+
+        @pl.when(late & (middle == 0))
         def near_now():
-            take(0, 1)
-
-        take(1, 1)
-        take(2, 1)
+            for i in rest:
+                take(0, i)
+
+        for i in rest:
+            take(1, i)
+            take(2, i)
+
+        @pl.when(late & (middle == 1))
+        def near_last():
+            for i in rest:
+                take(0, i)
 
     factor = QSCALE ** (-0.5) * LOG2E
     base = me // n
@@ -576,7 +583,8 @@
             step(c)
 
     run("turn", turn, 0)
-    run("relay", relay, 0)
+    with jax.named_scope("relay"):
+        relay()
     for c in range(1, len(CHUNKS) - 1):
         run("turn", turn, c)
     with jax.named_scope("relay_rest"):
@@ -584,9 +592,7 @@
     run("turn", turn, len(CHUNKS) - 1)
     for c in range(len(CHUNKS)):
         run("attend", attend, c)
-        if c > 1:
-            run("pair_up", pair_up, c - 2)
-    for c in range(len(CHUNKS) - 2, len(CHUNKS)):
+    for c in range(len(CHUNKS)):
         run("pair_up", pair_up, c)
     with jax.named_scope("drain"):
         drain()

time: 30.7 us -> 29.9 us (0.974)
  Pallas kernels: 28.6 us -> 27.8 us
    pallas_call x1, Pallas kernels: 28.6 us -> 27.8 us  [fused(): pl.pallas_call(functools.partial(fused_kernel, n), out_shape=jax.ShapeDty...]
where the time goes in v5:
time: 29.9 us; the launch traced here: 29.7 us
  Pallas kernels  27.8 us (93%)
  between operations  1.3 us (4%)
  local copies, waits for them, and re-layouts  0.63 us (2%)
    pallas_call x1, Pallas kernels, fused(): pl.pallas_call(functools.partial(fused_kernel, n), out_shape=jax.ShapeDty...  27.8 us
    unnamed x1, local copies, waits for them, and re-layouts  0.63 us

profile of v5, /device:TPU:0, one launch (start us, length us, event | category | flops | bytes accessed | tf_op | source)
XLA Modules:
  0.0 29.7 jit_solution(6968480118362434042)
XLA Ops:
  1.3 27.8 %shard_map.73 = bf16[8,4096]{1,0:T(8,128)(2,1)S(1)} custom-call(bf16[8,4096]{1,0:T(8,128)(2,1)} %q_hbm.1, bf16[8,2048]{1,0:T(8,128)(2,1)} %qk_hbm.1, bf16[8,2048]{1,0:T(8,128)(2,1)} %qv_hbm.1, bf16[512,2048]{1,0:T(8,128)(2,1)} %k_hbm.1, bf16[512,2048]{1,0:T(8,128)(2,1)} %v_hbm.1, s32[1]{0:T(128)S(6)} %copy.9.len_ref, s32[1]{0:T(128)S(6)} %copy.10.off_ref), custom_call_target="tpu_custom_call" | custom-call | tf_op jit(solution)/shard_map/pallas_call | solution.py:650
  29.1 0.6 %copy.11 = bf16[8,4096]{1,0:T(8,128)(2,1)} copy(bf16[8,4096]{1,0:T(8,128)(2,1)S(1)} %shard_map.73) | data formatting | bytes 131072
